TPU v7x, 32 devices: a whole 2x2x4 slice. The times are simulated.
32 devices in a mesh: seq: 4 (over y, x), ctx: 4 (over z), mp: 2 (over core).
Axes of the slice: x: 2, y: 2, z: 4, core: 2. Of those that a mesh axis runs over, the one named last changes fastest.
Arguments:
- tokens: bfloat16 [4, 512, 2048], P('seq', 'ctx'), may hold values from -5.75 to 6.25
- positions: int32 [4, 512], P('seq', 'ctx'), may hold values from 0 to 255, as said below
- routes: int32 [4, 512, 8], P('seq', 'ctx'), may hold values from 0 to 15, as said below
- cotangent: bfloat16 [4, 512, 2048], P('seq', 'ctx'), may hold values from -6 to 6
- attention_gain: bfloat16 [2048], P(('seq', 'ctx')), may hold values from 0.099609375 to 1.8984375
- query_weight: bfloat16 [2048, 2048], P(('seq', 'ctx'), 'mp'), may hold values from -0.125 to 0.125
- key_weight: bfloat16 [2048, 2048], P(('seq', 'ctx'), 'mp'), may hold values from -0.125 to 0.125
- value_weight: bfloat16 [2048, 2048], P(('seq', 'ctx'), 'mp'), may hold values from -0.125 to 0.125
- query_gain: bfloat16 [16, 128], P('mp', ('seq', 'ctx')), may hold values from 0.59765625 to 2
- key_gain: bfloat16 [16, 128], P('mp', ('seq', 'ctx')), may hold values from 0.59765625 to 2
- output_weight: bfloat16 [2048, 2048], P('mp', ('seq', 'ctx')), may hold values from -0.5 to 0.5
- ffn_gain: bfloat16 [2048], P(('seq', 'ctx')), may hold values from 0.099609375 to 1.8984375
- router_weight: bfloat16 [2048, 16], P(('seq', 'ctx')), may hold values from -0.093830323 to 0.06629126
- gate_weight: bfloat16 [16, 2048, 1024], P(('seq', 'ctx'), None, 'mp'), may hold values from -0.125 to 0.125
- up_weight: bfloat16 [16, 2048, 1024], P(('seq', 'ctx'), None, 'mp'), may hold values from -0.125 to 0.125
- down_weight: bfloat16 [16, 1024, 2048], P(('seq', 'ctx'), 'mp'), may hold values from -1.5 to 1.5
Outputs:
- layer_output: bfloat16 [4, 512, 2048], P('seq', 'ctx')
- tokens_grad: float32 [4, 512, 2048], P('seq', 'ctx')
- attention_gain_grad: float32 [2048], P(('seq', 'ctx'))
- query_weight_grad: float32 [2048, 2048], P(('seq', 'ctx'), 'mp')
- key_weight_grad: float32 [2048, 2048], P(('seq', 'ctx'), 'mp')
- value_weight_grad: float32 [2048, 2048], P(('seq', 'ctx'), 'mp')
- query_gain_grad: float32 [16, 128], P('mp', ('seq', 'ctx'))
- key_gain_grad: float32 [16, 128], P('mp', ('seq', 'ctx'))
- output_weight_grad: float32 [2048, 2048], P('mp', ('seq', 'ctx'))
- ffn_gain_grad: float32 [2048], P(('seq', 'ctx'))
- router_weight_grad: float32 [2048, 16], P(('seq', 'ctx'))
- gate_weight_grad: float32 [16, 2048, 1024], P(('seq', 'ctx'), None, 'mp')
- up_weight_grad: float32 [16, 2048, 1024], P(('seq', 'ctx'), None, 'mp')
- down_weight_grad: float32 [16, 1024, 2048], P(('seq', 'ctx'), 'mp')
Inputs may be any that keep to these rules, and one draw needn't show every extreme that they name: `positions`: within each sequence a position counts up by one from the previous token, or restarts at 0 where a packed document begins. Documents begin at the first token and at token 256, and nowhere else in the first half of a sequence. `routes`: each token names 8 different experts. Among the 1024 choices of one sequence block (one device's rows), no expert is named more than 96 times.
All inputs are finite; a program needn't handle non-finite values.
Results may differ from a plain program's by a relative error of at most 0.02.
Values may be sent and summed in bfloat16 or wider, within the bound.
A program may use at most 256 MiB of HBM per device.

v0:
```python
import jax
import jax.numpy as jnp
from jax import lax
from jax.sharding import PartitionSpec as P

HEADS = 16
HEAD_DIM = 128


eps = 1e-05
neg_big = -1e30


def rms_scale(rows, gain):
    return rows * lax.rsqrt(jnp.mean(rows * rows, axis=-1, keepdims=True) + eps) * gain


def rope_tables(positions):
    half = HEAD_DIM // 2
    freq = 10000.0 ** (-(jnp.arange(half).astype(jnp.float32) * 2.0 / HEAD_DIM))
    angle = positions.astype(jnp.float32)[:, None] * freq[None, :]
    return (jnp.cos(angle), jnp.sin(angle))


def rope_turn(normed, cosine, sine, factor):
    count = normed.shape[0]
    heads = normed.shape[1]
    width = normed.shape[2]
    first = normed[..., : width // 2]
    second = normed[..., width // 2 :]
    cos_rows = cosine[:, None, :]
    sin_rows = sine[:, None, :]
    turned = jnp.concatenate(
        [first * cos_rows - second * sin_rows, second * cos_rows + first * sin_rows], axis=-1
    )
    return (turned * factor).reshape(count, heads * width)


def contract_last(left, right):
    return lax.dot_general(
        left, right, (((1,), (1,)), ((), ())), preferred_element_type=jnp.float32
    )


def contract_first(left, right):
    return lax.dot_general(
        left, right, (((0,), (0,)), ((), ())), preferred_element_type=jnp.float32
    )


def sum_halves(part):
    return lax.psum(part.astype(jnp.bfloat16), "mp").astype(jnp.float32)


def body(
    tokens,
    positions,
    routes,
    cotangent,
    attention_gain,
    query_weight,
    key_weight,
    value_weight,
    query_gain,
    key_gain,
    output_weight,
    ffn_gain,
    router_weight,
    gate_weight,
    up_weight,
    down_weight,
):
    gathered = (
        lax.all_gather(query_weight, ("seq", "ctx"), axis=0, tiled=True),
        lax.all_gather(key_weight, ("seq", "ctx"), axis=0, tiled=True),
        lax.all_gather(value_weight, ("seq", "ctx"), axis=0, tiled=True),
        lax.all_gather(output_weight, ("seq", "ctx"), axis=1, tiled=True),
        lax.all_gather(router_weight, ("seq", "ctx"), axis=0, tiled=True),
        lax.all_gather(attention_gain, ("seq", "ctx"), axis=0, tiled=True),
        lax.all_gather(ffn_gain, ("seq", "ctx"), axis=0, tiled=True),
        lax.all_gather(query_gain, ("seq", "ctx"), axis=1, tiled=True),
        lax.all_gather(key_gain, ("seq", "ctx"), axis=1, tiled=True),
    )
    (
        query_full,
        key_full,
        value_full,
        output_full,
        router_full,
        gain_one_half,
        gain_two_half,
        query_gain_full,
        key_gain_full,
    ) = gathered
    rows = tokens.shape[1]
    width = tokens.shape[2]
    heads_here = query_gain.shape[0]
    local_width = query_weight.shape[1]
    all_columns = HEADS * HEAD_DIM
    factor = HEAD_DIM ** (-0.5)
    flat = tokens[0].astype(jnp.float32)
    grad_top = cotangent[0].astype(jnp.float32)
    gain_one = gain_one_half.astype(jnp.float32)
    gain_two = gain_two_half.astype(jnp.float32)
    query_gain_f = query_gain_full.astype(jnp.float32)
    key_gain_f = key_gain_full.astype(jnp.float32)
    normed_one = rms_scale(flat, gain_one).astype(jnp.bfloat16)
    query_raw = jnp.dot(normed_one, query_full, preferred_element_type=jnp.float32)
    key_raw = jnp.dot(normed_one, key_full, preferred_element_type=jnp.float32)
    value_rows = jnp.dot(normed_one, value_full, preferred_element_type=jnp.float32).astype(
        jnp.bfloat16
    )
    query_sq, key_sq = lax.psum(
        (jnp.sum(query_raw * query_raw, axis=-1), jnp.sum(key_raw * key_raw, axis=-1)), "mp"
    )
    query_inv = lax.rsqrt(query_sq / all_columns + eps)
    key_inv = lax.rsqrt(key_sq / all_columns + eps)
    query_unit = (query_raw * query_inv[:, None]).reshape(rows, heads_here, HEAD_DIM)
    key_unit = (key_raw * key_inv[:, None]).reshape(rows, heads_here, HEAD_DIM)
    cosine, sine = rope_tables(positions[0])
    query_rows = rope_turn(query_unit * query_gain_f, cosine, sine, factor).astype(jnp.bfloat16)
    key_rows = rope_turn(key_unit * key_gain_f, cosine, sine, 1.0).astype(jnp.bfloat16)
    keys_all, values_all = (
        lax.all_gather(key_rows, "ctx", axis=0, tiled=True),
        lax.all_gather(value_rows, "ctx", axis=0, tiled=True),
    )
    ctx_count = lax.axis_size("ctx")
    length = rows * ctx_count
    first_row = lax.axis_index("ctx") * rows
    last_row = first_row + rows - 1
    query_pos = first_row + jnp.arange(rows, dtype=jnp.int32)
    block = min(512, length)
    blocks = length // block
    query3 = query_rows.reshape(rows, heads_here, HEAD_DIM)

    def forward_block(carry, index):
        start = index * block

        def forward_work(state):
            top, total, acc = state
            keys = lax.dynamic_slice_in_dim(keys_all, start, block, 0).reshape(
                block, heads_here, HEAD_DIM
            )
            values = lax.dynamic_slice_in_dim(values_all, start, block, 0).reshape(
                block, heads_here, HEAD_DIM
            )
            scores = jnp.einsum("qhd,khd->hqk", query3, keys, preferred_element_type=jnp.float32)
            allowed = (start + jnp.arange(block, dtype=jnp.int32))[None, :] <= query_pos[:, None]
            scores = jnp.where(allowed[None], scores, neg_big)
            new_top = jnp.maximum(top, jnp.max(scores, axis=-1))
            weights = jnp.where(allowed[None], jnp.exp(scores - new_top[..., None]), 0.0)
            fade = jnp.exp(top - new_top)
            total = total * fade + jnp.sum(weights, axis=-1)
            acc = acc * fade[..., None] + jnp.einsum(
                "hqk,khd->hqd",
                weights.astype(jnp.bfloat16),
                values,
                preferred_element_type=jnp.float32,
            )
            return (new_top, total, acc)

        return (lax.cond(start <= last_row, forward_work, lambda state: state, carry), None)

    start_state = (
        jnp.full((heads_here, rows), neg_big, jnp.float32),
        jnp.zeros((heads_here, rows), jnp.float32),
        jnp.zeros((heads_here, rows, HEAD_DIM), jnp.float32),
    )
    (top, total, acc), _ = lax.scan(forward_block, start_state, jnp.arange(blocks, dtype=jnp.int32))
    mixed = (
        (acc / total[..., None]).transpose(1, 0, 2).reshape(rows, local_width).astype(jnp.bfloat16)
    )
    lse = top + jnp.log(total)
    attn = lax.psum(jnp.dot(mixed, output_full, preferred_element_type=jnp.float32), "mp")
    hidden = flat + attn
    normed_two = rms_scale(hidden, gain_two).astype(jnp.bfloat16)
    logits = jnp.dot(normed_two, router_full, preferred_element_type=jnp.float32)
    probs = jax.nn.softmax(logits, axis=-1)
    route_rows = routes[0]
    experts = router_full.shape[1]
    top_count = route_rows.shape[1]
    choose = (route_rows[:, :, None] == jnp.arange(experts, dtype=jnp.int32)[None, None, :]).astype(
        jnp.float32
    )
    share = jnp.sum(choose * probs[:, None, :], axis=-1)
    assign = rows * top_count
    capacity = assign * 3 // (2 * experts)
    expert_of = route_rows.reshape(assign)
    onehot = (expert_of[:, None] == jnp.arange(experts, dtype=jnp.int32)[None, :]).astype(jnp.int32)
    rank = jnp.sum(onehot * jnp.cumsum(onehot, axis=0), axis=1) - 1
    place = expert_of * capacity + rank
    table = (
        jnp.full((experts * capacity,), assign, jnp.int32)
        .at[place]
        .set(jnp.arange(assign, dtype=jnp.int32))
    )
    valid = table < assign
    safe = jnp.minimum(table, assign - 1)
    outgoing = jnp.where(
        valid[:, None], normed_two[safe // top_count], jnp.zeros((), jnp.bfloat16)
    ).reshape(experts, capacity, width)
    gate_here = gate_weight[0]
    up_here = up_weight[0]
    down_here = down_weight[0]
    received = lax.all_to_all(outgoing, ("seq", "ctx"), split_axis=0, concat_axis=0, tiled=True)
    sources = received.shape[0]
    slots = received.shape[1]
    inputs = received.reshape(sources * slots, width)
    gate = jnp.dot(inputs, gate_here, preferred_element_type=jnp.float32)
    up = jnp.dot(inputs, up_here, preferred_element_type=jnp.float32)
    act = (gate * jax.nn.sigmoid(gate) * up).astype(jnp.bfloat16)
    result = jnp.dot(act, down_here, preferred_element_type=jnp.float32).reshape(
        sources, slots, width
    )
    result = sum_halves(result)
    returned = lax.all_to_all(
        result.astype(jnp.bfloat16), ("seq", "ctx"), split_axis=0, concat_axis=0, tiled=True
    ).astype(result.dtype)
    per_assign = returned.reshape(experts * capacity, width)[place].reshape(rows, top_count, width)
    combined = jnp.sum(share[:, :, None] * per_assign, axis=1)
    layer_output = (hidden + combined).astype(jnp.bfloat16)[None]
    grad_share_part = jnp.sum(per_assign * grad_top[:, None, :], axis=-1)
    grad_result = (
        (share[:, :, None] * grad_top[:, None, :]).astype(jnp.bfloat16).reshape(assign, width)
    )
    grad_slots = jnp.where(valid[:, None], grad_result[safe], jnp.zeros((), jnp.bfloat16)).reshape(
        experts, capacity, width
    )
    incoming_rows, incoming_grads = (
        lax.all_to_all(outgoing, ("seq", "ctx"), split_axis=0, concat_axis=0, tiled=True),
        lax.all_to_all(grad_slots, ("seq", "ctx"), split_axis=0, concat_axis=0, tiled=True),
    )
    sources = incoming_rows.shape[0]
    inputs = incoming_rows.reshape(sources * capacity, width)
    grads_in = incoming_grads.reshape(sources * capacity, width)
    gate = jnp.dot(inputs, gate_here, preferred_element_type=jnp.float32)
    up = jnp.dot(inputs, up_here, preferred_element_type=jnp.float32)
    sig = jax.nn.sigmoid(gate)
    act = (gate * sig * up).astype(jnp.bfloat16)
    grad_act = contract_last(grads_in, down_here)
    down_grad = contract_first(act, grads_in)
    grad_gate = (grad_act * up * sig * (1.0 + gate * (1.0 - sig))).astype(jnp.bfloat16)
    grad_up = (grad_act * gate * sig).astype(jnp.bfloat16)
    gate_grad = contract_first(inputs, grad_gate)
    up_grad = contract_first(inputs, grad_up)
    back = (contract_last(grad_gate, gate_here) + contract_last(grad_up, up_here)).reshape(
        sources, capacity, width
    )
    back_home = lax.all_to_all(
        back.astype(jnp.bfloat16), ("seq", "ctx"), split_axis=0, concat_axis=0, tiled=True
    ).astype(back.dtype)
    moe_part = jnp.sum(
        back_home.reshape(experts * capacity, width)[place].reshape(rows, top_count, width), axis=1
    )
    share_send = jnp.zeros_like(grad_share_part)
    grad_norm_moe, share_summed = lax.psum((moe_part, share_send), "mp")
    grad_share = grad_share_part + share_summed
    grad_prob = jnp.sum(choose * grad_share[:, :, None], axis=1)
    grad_logits = (probs * (grad_prob - jnp.sum(probs * grad_prob, axis=-1, keepdims=True))).astype(
        jnp.bfloat16
    )
    router_grad = contract_first(normed_two, grad_logits)
    grad_normed_two = grad_norm_moe + contract_last(grad_logits, router_full)
    _, pull_two = jax.vjp(rms_scale, hidden, gain_two)
    grad_hidden_part, ffn_gain_grad = pull_two(grad_normed_two)
    grad_hidden = grad_top + grad_hidden_part
    grad_attn = grad_hidden.astype(jnp.bfloat16)
    output_grad = contract_first(mixed, grad_attn)
    grad_mixed = contract_last(grad_attn, output_full).astype(jnp.bfloat16)
    grad3 = grad_mixed.reshape(rows, heads_here, HEAD_DIM)
    delta = jnp.sum(
        grad3.astype(jnp.float32) * mixed.reshape(rows, heads_here, HEAD_DIM).astype(jnp.float32),
        axis=-1,
    ).T

    def backward_block(query_acc, index):
        start = index * block

        def backward_work(acc_now):
            keys = lax.dynamic_slice_in_dim(keys_all, start, block, 0).reshape(
                block, heads_here, HEAD_DIM
            )
            values = lax.dynamic_slice_in_dim(values_all, start, block, 0).reshape(
                block, heads_here, HEAD_DIM
            )
            scores = jnp.einsum("qhd,khd->hqk", query3, keys, preferred_element_type=jnp.float32)
            allowed = (start + jnp.arange(block, dtype=jnp.int32))[None, :] <= query_pos[:, None]
            scores = jnp.where(allowed[None], scores, neg_big)
            prob = jnp.where(allowed[None], jnp.exp(scores - lse[..., None]), 0.0)
            value_part = jnp.einsum(
                "hqk,qhd->khd", prob.astype(jnp.bfloat16), grad3, preferred_element_type=jnp.float32
            )
            grad_prob_block = jnp.einsum(
                "qhd,khd->hqk", grad3, values, preferred_element_type=jnp.float32
            )
            grad_scores = (prob * (grad_prob_block - delta[..., None])).astype(jnp.bfloat16)
            acc_now = acc_now + jnp.einsum(
                "hqk,khd->hqd", grad_scores, keys, preferred_element_type=jnp.float32
            )
            key_part = jnp.einsum(
                "hqk,qhd->khd", grad_scores, query3, preferred_element_type=jnp.float32
            )
            return (
                acc_now,
                key_part.reshape(block, local_width),
                value_part.reshape(block, local_width),
            )

        def skip(acc_now):
            empty = jnp.zeros((block, local_width), jnp.float32)
            return (acc_now, empty, empty)

        acc_next, key_part, value_part = lax.cond(start <= last_row, backward_work, skip, query_acc)
        return (acc_next, (key_part, value_part))

    query_acc, (key_blocks, value_blocks) = lax.scan(
        backward_block,
        jnp.zeros((heads_here, rows, HEAD_DIM), jnp.float32),
        jnp.arange(blocks, dtype=jnp.int32),
    )
    grad_keys, grad_values = (
        lax.psum_scatter(
            key_blocks.reshape(length, local_width).astype(jnp.bfloat16),
            "ctx",
            scatter_dimension=0,
            tiled=True,
        ).astype(jnp.float32),
        lax.psum_scatter(
            value_blocks.reshape(length, local_width).astype(jnp.bfloat16),
            "ctx",
            scatter_dimension=0,
            tiled=True,
        ).astype(jnp.float32),
    )
    grad_queries = query_acc.transpose(1, 0, 2).reshape(rows, local_width)
    _, pull_query = jax.vjp(
        lambda normed: rope_turn(normed, cosine, sine, factor), query_unit * query_gain_f
    )
    (grad_query_normed,) = pull_query(grad_queries)
    _, pull_key = jax.vjp(
        lambda normed: rope_turn(normed, cosine, sine, 1.0), key_unit * key_gain_f
    )
    (grad_key_normed,) = pull_key(grad_keys)
    query_gain_grad = jnp.sum(grad_query_normed * query_unit, axis=0)
    key_gain_grad = jnp.sum(grad_key_normed * key_unit, axis=0)
    query_scaled = (grad_query_normed * query_gain_f).reshape(rows, local_width)
    key_scaled = (grad_key_normed * key_gain_f).reshape(rows, local_width)
    query_dot, key_dot = lax.psum(
        (jnp.sum(query_raw * query_scaled, axis=-1), jnp.sum(key_raw * key_scaled, axis=-1)), "mp"
    )
    grad_query_raw = (
        query_inv[:, None] * query_scaled
        - query_raw * (query_inv * query_inv * query_inv * query_dot / all_columns)[:, None]
    )
    grad_key_raw = (
        key_inv[:, None] * key_scaled
        - key_raw * (key_inv * key_inv * key_inv * key_dot / all_columns)[:, None]
    )
    query_half = grad_query_raw.astype(jnp.bfloat16)
    key_half = grad_key_raw.astype(jnp.bfloat16)
    value_half = grad_values.astype(jnp.bfloat16)
    query_grad = contract_first(normed_one, query_half)
    key_grad = contract_first(normed_one, key_half)
    value_grad = contract_first(normed_one, value_half)
    normed_part = (
        contract_last(query_half, query_full)
        + contract_last(key_half, key_full)
        + contract_last(value_half, value_full)
    )
    grad_normed_one = lax.psum(normed_part.astype(jnp.bfloat16), "mp").astype(jnp.float32)
    _, pull_one = jax.vjp(rms_scale, flat, gain_one)
    grad_flat_part, attention_gain_grad = pull_one(grad_normed_one)
    tokens_grad = (grad_hidden + grad_flat_part)[None]
    owned = (
        lax.psum_scatter(query_grad, ("seq", "ctx"), scatter_dimension=0, tiled=True),
        lax.psum_scatter(key_grad, ("seq", "ctx"), scatter_dimension=0, tiled=True),
        lax.psum_scatter(value_grad, ("seq", "ctx"), scatter_dimension=0, tiled=True),
        lax.psum_scatter(output_grad, ("seq", "ctx"), scatter_dimension=1, tiled=True),
        lax.psum_scatter(router_grad, ("seq", "ctx"), scatter_dimension=0, tiled=True),
        lax.psum_scatter(attention_gain_grad, ("seq", "ctx"), scatter_dimension=0, tiled=True),
        lax.psum_scatter(ffn_gain_grad, ("seq", "ctx"), scatter_dimension=0, tiled=True),
        lax.psum_scatter(query_gain_grad, ("seq", "ctx"), scatter_dimension=1, tiled=True),
        lax.psum_scatter(key_gain_grad, ("seq", "ctx"), scatter_dimension=1, tiled=True),
    )
    (
        query_owned,
        key_owned,
        value_owned,
        output_owned,
        router_owned,
        gain_one_owned,
        gain_two_owned,
        query_gain_owned,
        key_gain_owned,
    ) = owned
    return (
        layer_output,
        tokens_grad,
        gain_one_owned,
        query_owned,
        key_owned,
        value_owned,
        query_gain_owned,
        key_gain_owned,
        output_owned,
        gain_two_owned,
        router_owned,
        gate_grad[None],
        up_grad[None],
        down_grad[None],
    )


def solution(mesh):
    placed = (
        P("seq", "ctx", None),
        P("seq", "ctx"),
        P("seq", "ctx", None),
        P("seq", "ctx", None),
        P(("seq", "ctx")),
        P(("seq", "ctx"), "mp"),
        P(("seq", "ctx"), "mp"),
        P(("seq", "ctx"), "mp"),
        P("mp", ("seq", "ctx")),
        P("mp", ("seq", "ctx")),
        P("mp", ("seq", "ctx")),
        P(("seq", "ctx")),
        P(("seq", "ctx"), None),
        P(("seq", "ctx"), None, "mp"),
        P(("seq", "ctx"), None, "mp"),
        P(("seq", "ctx"), "mp", None),
    )
    return jax.shard_map(
        body,
        mesh=mesh,
        in_specs=placed,
        out_specs=(
            P("seq", "ctx", None),
            P("seq", "ctx", None),
            P(("seq", "ctx")),
            P(("seq", "ctx"), "mp"),
            P(("seq", "ctx"), "mp"),
            P(("seq", "ctx"), "mp"),
            P("mp", ("seq", "ctx")),
            P("mp", ("seq", "ctx")),
            P("mp", ("seq", "ctx")),
            P(("seq", "ctx")),
            P(("seq", "ctx"), None),
            P(("seq", "ctx"), None, "mp"),
            P(("seq", "ctx"), None, "mp"),
            P(("seq", "ctx"), "mp", None),
        ),
        check_vma=False,
    )
```

profile of v0, /device:TPU:12, one launch (start us, length us, event | category | flops | bytes accessed | tf_op | source)
XLA Modules:
  0.0 2041.3 jit_solution(13428913090188975238)
XLA Ops:
  11.0 36.2 %all-gather = bf16[16,1,128]{2,1,0:T(2,128)(2,1)S(1)} all-gather(bf16[1,1,128]{2,1,0:T(2,128)(2,1)} %bitcast.234), channel_id=1, replica_groups=mesh['seq'=4,'ctx'=4,'mp'=2] {'seq','ctx'}, dimensions={0}, use_global_device_ids=true | all-gather | bytes 4352 | tf_op jit(solution)/shard_map/all_gather | solution.py:79
  47.2 41.2 %all_gather.35 = bf16[8,128]{0,1:T(8,128)(2,1)S(1)} all-gather(bf16[8,8]{0,1:T(8,128)(2,1)S(1)} %copy.180), channel_id=1, replica_groups=mesh['seq'=4,'ctx'=4,'mp'=2] {'seq','ctx'}, dimensions={1}, use_global_device_ids=true | all-gather | bytes 2176 | tf_op jit(solution)/shard_map/all_gather | solution.py:82
  88.5 36.1 %all_gather.38 = bf16[8,128]{0,1:T(8,128)(2,1)S(1)} all-gather(bf16[8,8]{0,1:T(8,128)(2,1)S(1)} %copy.183), channel_id=1, replica_groups=mesh['seq'=4,'ctx'=4,'mp'=2] {'seq','ctx'}, dimensions={1}, use_global_device_ids=true | all-gather | bytes 2176 | tf_op jit(solution)/shard_map/all_gather | solution.py:81
  127.3 3.8 convolution_convert_fusion.2
  131.2 33.7 %all-gather.13.cloned.1.call-done = bf16[2048,1024]{1,0:T(8,128)(2,1)} async-done(((bf16[128,1024]{1,0:T(8,128)(2,1)}), bf16[2048,1024]{1,0:T(8,128)(2,1)}) %all-gather.13.cloned.1.call-update) | async-done | bytes 4194320 | tf_op jit(solution)/shard_map/all_gather | solution.py:74
  164.9 3.0 multiply_reduce_fusion.8
  167.9 73.9 %all-gather.9.cloned.1.call-done = bf16[2048,1024]{1,0:T(8,128)(2,1)} async-done(((bf16[128,1024]{1,0:T(8,128)(2,1)}), bf16[2048,1024]{1,0:T(8,128)(2,1)}) %all-gather.9.cloned.1.call-update) | async-done | bytes 4194320 | tf_op jit(solution)/shard_map/all_gather | solution.py:75
  241.9 3.7 multiply_reduce_fusion.9
  245.6 2.4 all-reduce.10
  259.5 36.5 %all-gather.1 = bf16[16,1,128]{2,1,0:T(2,128)(2,1)S(1)} all-gather(bf16[1,1,128]{2,1,0:T(2,128)(2,1)S(1)} %bitcast.235), channel_id=1, replica_groups=mesh['seq'=4,'ctx'=4,'mp'=2] {'seq','ctx'}, dimensions={0}, use_global_device_ids=true | all-gather | bytes 4352 | tf_op jit(solution)/shard_map/all_gather | solution.py:80
  296.2 4.5 reduce-window.6
  301.2 4.3 scatter_custom_fusion
  307.6 5.4 conditional.2
  315.2 74.4 %all-gather.19.cloned.1.call-done = bf16[1024,2048]{1,0:T(8,128)(2,1)} async-done(((bf16[1024,128]{1,0:T(8,128)(2,1)}), bf16[1024,2048]{1,0:T(8,128)(2,1)}) %all-gather.19.cloned.1.call-update) | async-done | bytes 4194320 | tf_op jit(solution)/shard_map/all_gather | solution.py:77
  389.7 3.9 fusion.74
  393.7 38.5 %all_gather.43 = bf16[2048,16]{0,1:T(8,128)(2,1)S(1)} all-gather(bf16[128,16]{0,1:T(8,128)(2,1)S(1)} %copy-done.64), channel_id=1, replica_groups=mesh['seq'=4,'ctx'=4,'mp'=2] {'seq','ctx'}, dimensions={0}, use_global_device_ids=true | all-gather | bytes 69632 | tf_op jit(solution)/shard_map/all_gather | solution.py:78
  438.0 7.0 gather_fusion
  445.1 3.5 fusion.15
  448.6 15.5 gather_fusion.2
  464.1 8.2 broadcast_select_fusion
  472.3 135.8 %all_to_all.21 = bf16[16,96,2048]{2,1,0:T(8,128)(2,1)} all-to-all(bf16[16,96,2048]{2,1,0:T(8,128)(2,1)S(1)} %get-tuple-element.301), channel_id=1, replica_groups=mesh['seq'=4,'ctx'=4,'mp'=2] {'seq','ctx'}, dimensions={0} | all-to-all | bytes 12582912 | tf_op jit(solution)/shard_map/all_to_all | solution.py:205
  608.1 7.9 all-to-all-start.2
  616.0 8.7 fusion.23
  624.7 5.2 fusion.27
  629.9 122.2 %all-to-all-done.2 = bf16[16,96,2048]{2,1,0:T(8,128)(2,1)} async-done(((bf16[16,96,2048]{2,1,0:T(8,128)(2,1)}), bf16[16,96,2048]{2,1,0:T(8,128)(2,1)}, u32[]{:S(2)}, u32[]{:S(2)}) %all-to-all-start.2) | async-done | bytes 6291488 | tf_op jit(solution)/shard_map/all_to_all | solution.py:231
  752.1 9.7 multiply_convert_fusion.1
  761.8 6.5 fusion.25
  768.4 8.3 add_convert_fusion
  776.7 22.6 %all-to-all-start.3 = ((bf16[16,96,2048]{2,1,0:T(8,128)(2,1)}), bf16[16,96,2048]{2,1,0:T(8,128)(2,1)}, u32[]{:S(2)}, u32[]{:S(2)}) async-start(bf16[16,96,2048]{2,1,0:T(8,128)(2,1)} %bitcast.201), calls=%async_computation.3 | async-start | bytes 12582912 | tf_op jit(solution)/shard_map/all_to_all | solution.py:249
  799.3 12.0 all-reduce.18.cloned.1.call-start
  811.3 6.8 convolution_convert_fusion
  818.1 33.5 %all-reduce.18.cloned.1.call-done = bf16[16,96,2048]{2,1,0:T(8,128)(2,1)} async-done(((bf16[16,96,2048]{2,1,0:T(8,128)(2,1)}), bf16[16,96,2048]{2,1,0:T(8,128)(2,1)}) %all-reduce.18.cloned.1.call-update) | async-done | bytes 6291472 | tf_op jit(solution)/shard_map/psum | solution.py:52
  851.6 87.4 %all-to-all-done.3 = bf16[16,96,2048]{2,1,0:T(8,128)(2,1)} async-done(((bf16[16,96,2048]{2,1,0:T(8,128)(2,1)}), bf16[16,96,2048]{2,1,0:T(8,128)(2,1)}, u32[]{:S(2)}, u32[]{:S(2)}) %all-to-all-start.3) | async-done | bytes 6291488 | tf_op jit(solution)/shard_map/all_to_all | solution.py:249
  939.0 16.7 all-to-all-start.1
  955.8 8.9 bitcast_convert_fusion
  964.6 13.5 gather_fusion.3
  978.2 6.3 bitcast_reduce_fusion
  984.6 110.9 %all-to-all-done.1 = bf16[16,96,2048]{2,1,0:T(8,128)(2,1)} async-done(((bf16[16,96,2048]{2,1,0:T(8,128)(2,1)}), bf16[16,96,2048]{2,1,0:T(8,128)(2,1)}, u32[]{:S(2)}, u32[]{:S(2)}) %all-to-all-start.1) | async-done | bytes 6291488 | tf_op jit(solution)/shard_map/all_to_all | solution.py:216
  1095.5 8.9 bitcast_convert_fusion.1
  1104.4 13.6 gather_fusion.1
  1118.1 5.3 fusion.17
  1129.8 10.9 conditional.3
  1136.1 2.3 convolution_add_fusion.1
  1138.4 2.3 fusion.73
  1140.7 2.3 copy.215
  1144.4 2.3 copy.217
  1147.7 28.2 %reduce-scatter.24.cloned.1.call-done = bf16[128,1024]{1,0:T(8,128)(2,1)} async-done(((bf16[512,1024]{1,0:T(8,128)(2,1)}), bf16[128,1024]{1,0:T(8,128)(2,1)}) %reduce-scatter.24.cloned.1.call-update) | async-done | bytes 262160
  1183.2 2.7 all-reduce.9
  1186.8 4.2 fusion.75
  1192.5 12.0 reduce-scatter.26.cloned.1.call-done
  1204.6 4.6 fusion.18
  1210.2 4.5 fusion.43
  1215.9 4.6 fusion.61
  1220.6 4.7 fusion.63
  1226.2 4.6 fusion.65
  1233.3 7.9 convolution_bitcast_fusion
  1241.3 8.1 convolution_bitcast_fusion.1
  1249.5 5.0 convolution_bitcast_fusion.2
  1256.0 71.8 %all-reduce.8 = (f32[2048]{0:T(1024)S(1)}, f32[8,128]{1,0:T(8,128)S(1)}, f32[8,128]{1,0:T(8,128)S(1)}, f32[2048]{0:T(1024)S(1)}) all-reduce(f32[2048]{0:T(1024)S(1)} %get-tuple-element.261, f32[8,128]{1,0:T(8,128)S(1)} %get-tuple-element.292, ...), channel_id=4, replica_groups=mesh['seq'=4,'ctx'=4,'mp'=2] {'seq','ctx'}, use_global_device_ids=true, to_apply=%region_38.39.clone | all-reduce | flops 6144 | bytes 49152
  1330.4 2.6 fusion.36
  1333.0 153.4 %reduce-scatter.20.cloned.1.call-done = f32[1024,128]{1,0:T(8,128)} async-done(((f32[1024,2048]{1,0:T(8,128)}), f32[1024,128]{1,0:T(8,128)}) %reduce-scatter.20.cloned.1.call-update) | async-done | bytes 524304 | tf_op jit(solution)/shard_map/reduce_scatter | solution.py:378
  1486.4 182.7 %reduce-scatter.18.cloned.1.call-done = f32[128,1024]{1,0:T(8,128)} async-done(((f32[2048,1024]{1,0:T(8,128)}), f32[128,1024]{1,0:T(8,128)}) %reduce-scatter.18.cloned.1.call-update) | async-done | bytes 524304 | tf_op jit(solution)/shard_map/reduce_scatter | solution.py:377
  1669.2 182.6 %reduce-scatter.16.cloned.1.call-done = f32[128,1024]{1,0:T(8,128)} async-done(((f32[2048,1024]{1,0:T(8,128)}), f32[128,1024]{1,0:T(8,128)}) %reduce-scatter.16.cloned.1.call-update) | async-done | bytes 524304 | tf_op jit(solution)/shard_map/reduce_scatter | solution.py:376
  1851.8 182.6 %reduce-scatter.14.cloned.1.call-done = f32[128,1024]{1,0:T(8,128)} async-done(((f32[2048,1024]{1,0:T(8,128)}), f32[128,1024]{1,0:T(8,128)}) %reduce-scatter.14.cloned.1.call-update) | async-done | bytes 524304 | tf_op jit(solution)/shard_map/reduce_scatter | solution.py:375
  (321 shorter events, 66.9 us)
Async XLA Ops:
  7.2 744.9 %copy-start = (bf16[1,512,2048]{2,1,0:T(8,128)(2,1)S(1)}, bf16[1,512,2048]{2,1,0:T(8,128)(2,1)}, u32[]{:S(2)}) copy-start(bf16[1,512,2048]{2,1,0:T(8,128)(2,1)} %param.35) | copy-start | bytes 6291460
  7.2 157.7 %copy-start.4 = (bf16[1,128,2048]{2,1,0:T(8,128)(2,1)S(1)}, bf16[1,128,2048]{2,1,0:T(8,128)(2,1)}, u32[]{:S(2)}) copy-start(bf16[1,128,2048]{2,1,0:T(8,128)(2,1)} %param.20) | copy-start | bytes 1572868
  7.2 120.1 %all-gather.15.cloned.1.call-start = ((), (), s32[]{:S(2)}) async-start(), calls=%async_computation.14 | async-start | bytes 4456448 | tf_op jit(solution)/shard_map/all_gather | solution.py:76
  7.9 157.0 %all-gather.13.cloned.1.call-start = ((), (), s32[]{:S(2)}) async-start(), calls=%async_computation.13 | async-start | bytes 4456448 | tf_op jit(solution)/shard_map/all_gather | solution.py:74
  8.7 233.2 %all-gather.9.cloned.1.call-start = ((), (), s32[]{:S(2)}) async-start(), calls=%async_computation.11 | async-start | bytes 4456448 | tf_op jit(solution)/shard_map/all_gather | solution.py:75
  9.4 298.2 %all-gather.17.cloned.1.call-start = ((), (), s32[]{:S(2)}) async-start(), calls=%async_computation.15 | async-start | bytes 1310720 | tf_op jit(solution)/shard_map/all_gather | solution.py:125
  47.2 194.7 %copy-start.27 = (f32[16,1,128]{2,1,0:T(1,128)}, f32[16,1,128]{2,1,0:T(1,128)S(1)}, u32[]{:S(2)}) copy-start(f32[16,1,128]{2,1,0:T(1,128)S(1)} %convert_element_type.203) | copy-start | bytes 24580
  88.4 167.9 %copy-start.52 = (f32[8,128]{1,0:T(8,128)}, f32[8,128]{1,0:T(8,128)S(1)}, u32[]{:S(2)}) copy-start(f32[8,128]{1,0:T(8,128)S(1)} %convert_element_type.166) | copy-start | bytes 12292
  124.6 130.5 %copy-start.50 = (f32[8,128]{1,0:T(8,128)}, f32[8,128]{1,0:T(8,128)S(1)}, u32[]{:S(2)}) copy-start(f32[8,128]{1,0:T(8,128)S(1)} %convert_element_type.171) | copy-start | bytes 12292
  126.4 115.5 %copy-start.48 = (f32[128]{0:T(128)}, f32[128]{0:T(128)S(1)}, u32[]{:S(2)}) copy-start(f32[128]{0:T(128)S(1)} %fusion.59) | copy-start | bytes 1540
  127.2 130.4 %copy-start.36 = (f32[128,64]{0,1:T(8,128)}, f32[128,64]{0,1:T(8,128)S(1)}, u32[]{:S(2)}) copy-start(f32[128,64]{0,1:T(8,128)S(1)} %get-tuple-element.302) | copy-start | bytes 98308
  127.2 130.4 %copy-start.38 = (f32[128,64]{0,1:T(8,128)}, f32[128,64]{0,1:T(8,128)S(1)}, u32[]{:S(2)}) copy-start(f32[128,64]{0,1:T(8,128)S(1)} %get-tuple-element.303) | copy-start | bytes 98308
  131.1 176.5 %all-gather.11.cloned.1.call-start = ((), (), s32[]{:S(2)}) async-start(), calls=%async_computation.12 | async-start | bytes 1310720 | tf_op jit(solution)/shard_map/all_gather | solution.py:124
  167.9 85.1 %copy-start.12 = (f32[128,1024]{1,0:T(8,128)}, f32[128,1024]{1,0:T(8,128)S(1)}, u32[]{:S(2)}) copy-start(f32[128,1024]{1,0:T(8,128)S(1)} %get-tuple-element.307) | copy-start | bytes 1572868
  248.1 10.4 copy-start.68
  248.1 10.4 copy-start.70
  248.1 10.4 copy-start.60
  248.1 10.4 copy-start.62
  249.0 10.1 copy-start.46
  249.0 10.4 copy-start.67
  258.5 131.1 %all-gather.19.cloned.1.call-start = ((), (), s32[]{:S(2)}) async-start(), calls=%async_computation.16 | async-start | bytes 4456448 | tf_op jit(solution)/shard_map/all_gather | solution.py:77
  259.1 175.3 %all-reduce.16.cloned.1.call-start = ((), (), s32[]{:S(2)}) async-start(), calls=%async_computation.17 | async-start | bytes 2097152 | tf_op jit(solution)/shard_map/psum | solution.py:174
  295.9 139.9 %copy-start.42 = (f32[16,1,128]{2,1,0:T(1,128)}, f32[16,1,128]{2,1,0:T(1,128)S(1)}, u32[]{:S(2)}) copy-start(f32[16,1,128]{2,1,0:T(1,128)S(1)} %convert_element_type.204) | copy-start | bytes 24580
  313.9 79.8 %copy-start.64 = (bf16[128,16]{0,1:T(8,128)(2,1)S(1)}, bf16[128,16]{0,1:T(8,128)(2,1)}, u32[]{:S(2)}) copy-start(bf16[128,16]{0,1:T(8,128)(2,1)} %param.32) | copy-start | bytes 12292
  315.2 119.2 %copy-start.18 = (f32[8,128,128]{1,2,0:T(8,128)}, f32[8,128,128]{1,2,0:T(8,128)S(1)}, u32[]{:S(2)}) copy-start(f32[8,128,128]{1,2,0:T(8,128)S(1)} %copy.188) | copy-start | bytes 1572868
  315.2 120.6 %copy-start.21 = (bf16[8,128,128]{1,2,0:T(8,128)(2,1)}, bf16[8,128,128]{1,2,0:T(8,128)(2,1)S(1)}, u32[]{:S(2)}) copy-start(bf16[8,128,128]{1,2,0:T(8,128)(2,1)S(1)} %divide_convert_fusion) | copy-start | bytes 786436
  432.2 12.9 copy-start.32
  436.9 8.2 copy-start.2
  608.1 144.0 %all-to-all-start.2 = ((bf16[16,96,2048]{2,1,0:T(8,128)(2,1)}), bf16[16,96,2048]{2,1,0:T(8,128)(2,1)}, u32[]{:S(2)}, u32[]{:S(2)}) async-start(bf16[16,96,2048]{2,1,0:T(8,128)(2,1)} %get-tuple-element.300), calls=%async_computation.2 | async-start | bytes 12582912 | tf_op jit(solution)/shard_map/all_to_all | solution.py:231
  616.0 8.7 copy-start.15
  616.0 8.7 copy-start.74
  752.1 9.7 copy-start.75
  776.7 162.3 %all-to-all-start.3 = ((bf16[16,96,2048]{2,1,0:T(8,128)(2,1)}), bf16[16,96,2048]{2,1,0:T(8,128)(2,1)}, u32[]{:S(2)}, u32[]{:S(2)}) async-start(bf16[16,96,2048]{2,1,0:T(8,128)(2,1)} %bitcast.201), calls=%async_computation.3 | async-start | bytes 12582912 | tf_op jit(solution)/shard_map/all_to_all | solution.py:249
  799.3 52.3 %all-reduce.18.cloned.1.call-start = ((), (), s32[]{:S(2)}) async-start(), calls=%async_computation.18 | async-start | bytes 12582912 | tf_op jit(solution)/shard_map/psum | solution.py:52
  939.0 156.5 %all-to-all-start.1 = ((bf16[16,96,2048]{2,1,0:T(8,128)(2,1)}), bf16[16,96,2048]{2,1,0:T(8,128)(2,1)}, u32[]{:S(2)}, u32[]{:S(2)}) async-start(bf16[16,96,2048]{2,1,0:T(8,128)(2,1)} %all-reduce.18.cloned.1.call-done), calls=%async_computation.1 | async-start | bytes 12582912 | tf_op jit(solution)/shard_map/all_to_all | solution.py:216
  955.7 167.9 %all-reduce.20.cloned.1.call-start = ((), (), s32[]{:S(2)}) async-start(), calls=%async_computation.19 | async-start | bytes 2097152 | tf_op jit(solution)/shard_map/psum | solution.py:256
  984.5 191.4 %reduce-scatter.24.cloned.1.call-start = ((), (), s32[]{:S(2)}) async-start(), calls=%async_computation.26 | async-start | bytes 1310720
  1104.4 13.6 copy-start.11
  1104.4 13.6 copy-start.35
  1127.8 82.4 %copy-start.10 = (f32[128,2048]{1,0:T(8,128)}, f32[128,2048]{1,0:T(8,128)S(1)}, u32[]{:S(2)}) copy-start(f32[128,2048]{1,0:T(8,128)S(1)} %get-tuple-element.280) | copy-start | bytes 3145732
  1143.0 34.1 %copy-start.37 = (f32[128,64]{0,1:T(8,128)S(1)}, f32[128,64]{0,1:T(8,128)}, u32[]{:S(2)}) copy-start(f32[128,64]{0,1:T(8,128)} %copy-done.36) | copy-start | bytes 98308
  1143.0 34.1 %copy-start.39 = (f32[128,64]{0,1:T(8,128)S(1)}, f32[128,64]{0,1:T(8,128)}, u32[]{:S(2)}) copy-start(f32[128,64]{0,1:T(8,128)} %copy-done.38) | copy-start | bytes 98308
  1143.0 61.5 %reduce-scatter.26.cloned.1.call-start = ((), (), s32[]{:S(2)}) async-start(), calls=%async_computation.27 | async-start | bytes 1310720
  1143.1 35.3 %copy-start.17 = (f32[128,1024]{0,1:T(8,128)S(1)}, f32[128,1024]{0,1:T(8,128)}, u32[]{:S(2)}) copy-start(f32[128,1024]{0,1:T(8,128)} %copy.223) | copy-start | bytes 1572868
  1143.1 35.3 %copy-start.53 = (f32[8,128]{1,0:T(8,128)S(1)}, f32[8,128]{1,0:T(8,128)}, u32[]{:S(2)}) copy-start(f32[8,128]{1,0:T(8,128)} %copy-done.52) | copy-start | bytes 12292
  1144.4 35.0 %copy-start.16 = (f32[128,1024]{0,1:T(8,128)S(1)}, f32[128,1024]{0,1:T(8,128)}, u32[]{:S(2)}) copy-start(f32[128,1024]{0,1:T(8,128)} %copy.224) | copy-start | bytes 1572868
  1144.4 35.0 %copy-start.51 = (f32[8,128]{1,0:T(8,128)S(1)}, f32[8,128]{1,0:T(8,128)}, u32[]{:S(2)}) copy-start(f32[8,128]{1,0:T(8,128)} %copy-done.50) | copy-start | bytes 12292
  1147.6 106.8 %all-reduce.22.cloned.1.call-start = ((), (), s32[]{:S(2)}) async-start(), calls=%async_computation.20 | async-start | bytes 1048576 | tf_op jit(solution)/shard_map/psum | solution.py:370
  1178.4 7.5 copy-start.69
  1178.4 7.5 copy-start.63
  1178.4 7.6 copy-start.61
  1192.5 16.7 copy-start.3
  1192.5 17.7 copy-start.22
  1209.2 123.8 %reduce-scatter.22.cloned.1.call-start = ((), (), s32[]{:S(2)}) async-start(), calls=%async_computation.25 | async-start | bytes 139264 | tf_op jit(solution)/shard_map/reduce_scatter | solution.py:379
  1210.1 276.3 %reduce-scatter.20.cloned.1.call-start = ((), (), s32[]{:S(2)}) async-start(), calls=%async_computation.24 | async-start | bytes 8912896 | tf_op jit(solution)/shard_map/reduce_scatter | solution.py:378
  1214.8 454.4 %reduce-scatter.18.cloned.1.call-start = ((), (), s32[]{:S(2)}) async-start(), calls=%async_computation.23 | async-start | bytes 8912896 | tf_op jit(solution)/shard_map/reduce_scatter | solution.py:377
  1220.5 631.3 %reduce-scatter.16.cloned.1.call-start = ((), (), s32[]{:S(2)}) async-start(), calls=%async_computation.22 | async-start | bytes 8912896 | tf_op jit(solution)/shard_map/reduce_scatter | solution.py:376
  1225.2 809.1 %reduce-scatter.14.cloned.1.call-start = ((), (), s32[]{:S(2)}) async-start(), calls=%async_computation.21 | async-start | bytes 8912896 | tf_op jit(solution)/shard_map/reduce_scatter | solution.py:375
  1233.3 8.0 copy-start.80
  1233.3 16.1 slice-start
  1241.3 8.1 slice-start.1
  1241.3 8.1 copy-start.82
  1249.4 80.9 %copy-start.66 = (f32[128]{0:T(128)S(1)}, f32[128]{0:T(128)}, u32[]{:S(2)}) copy-start(f32[128]{0:T(128)} %copy-done.65) | copy-start | bytes 1540
  1249.4 784.9 %copy-start.1 = (bf16[1,512,2048]{2,1,0:T(8,128)(2,1)S(1)}, bf16[1,512,2048]{2,1,0:T(8,128)(2,1)}, u32[]{:S(2)}) copy-start(bf16[1,512,2048]{2,1,0:T(8,128)(2,1)} %param.35) | copy-start | bytes 6291460
  (41 other events, 137.6 us)
Sparse Core Ops, SparseCore 0:
  10.8 77.0 all-gather.14
  90.6 74.2 all-gather.12
  167.7 74.1 all-gather.8
  243.9 26.5 all-gather.16
  272.5 27.5 all-gather.10
  302.7 86.9 all-gather.18
  393.7 19.7 all-reduce.15
  818.2 33.3 all-reduce.17
  984.6 20.5 all-reduce.19
  1143.2 32.6 reduce-scatter.23
  1178.8 25.7 reduce-scatter.25
  1209.3 19.4 all-reduce.21
  1231.6 73.2 reduce-scatter.21
  1307.7 178.7 reduce-scatter.19
  1489.1 179.9 reduce-scatter.17
  1671.9 179.8 reduce-scatter.15
  1854.5 179.8 reduce-scatter.13
where the time goes:
time: 2050 us; the launch traced here: 2040 us
  waiting for transfers between devices  1280 us (62%)
  blocking collectives  401 us (20%)
  matrix products  127 us (6%)
  local copies, waits for them, and re-layouts  82.7 us (4%)
  other arithmetic  72.8 us (4%)
  starting transfers between devices  60.2 us (3%)
    reduce_scatter x1, waiting for transfers between devices, body(): lax.psum_scatter(value_grad, ('seq', 'ctx'), scatter_dimension=0, tiled=T...  183 us
    reduce_scatter x1, waiting for transfers between devices, body(): lax.psum_scatter(key_grad, ('seq', 'ctx'), scatter_dimension=0, tiled=True)  183 us
    reduce_scatter x1, waiting for transfers between devices, body(): lax.psum_scatter(query_grad, ('seq', 'ctx'), scatter_dimension=0, tiled=T...  183 us
    reduce_scatter x1, waiting for transfers between devices, body(): lax.psum_scatter(output_grad, ('seq', 'ctx'), scatter_dimension=1, tiled=...  153 us
    all_to_all x1, blocking collectives, body(): lax.all_to_all(outgoing, ('seq', 'ctx'), split_axis=0, concat_axis=0, til...  136 us
    all_to_all x1, waiting for transfers between devices, body(): lax.all_to_all(grad_slots, ('seq', 'ctx'), split_axis=0, concat_axis=0, t...  122 us
    all_to_all x1, waiting for transfers between devices, body(): lax.all_to_all(result.astype(jnp.bfloat16), ('seq', 'ctx'), split_axis=0,...  111 us
    all_to_all x1, waiting for transfers between devices, body(): lax.all_to_all(back.astype(jnp.bfloat16), ('seq', 'ctx'), split_axis=0, c...  87.4 us
  transfers between devices with their start and end apart: 20, of which 13 were waited for; matrix products, arithmetic and copies ran while one was open for 9% of the time, Pallas kernels for 0%

commit v1 on v0

--- a/solution.py
+++ b/solution.py
@@ -1,7 +1,1487 @@
+import functools
+
 import jax
 import jax.numpy as jnp
+import numpy as np
 from jax import lax
+from jax.experimental import pallas as pl
+from jax.experimental.pallas import tpu as pltpu
 from jax.sharding import PartitionSpec as P
+
+MESH = pl.DeviceIdType.MESH
+BF = jnp.bfloat16
+F32 = jnp.float32
+
+
+def place():
+    s = lax.axis_index("seq")
+    z = lax.axis_index("ctx")
+    m = lax.axis_index("mp")
+    return s, z, m
+
+
+def flip_x(s):
+    return s + 1 - 2 * lax.rem(s, 2)
+
+
+def flip_y(s):
+    return s + 2 - 4 * lax.div(s, 2)
+
+
+def remote(src, dst, send, recv, device):
+    return pltpu.make_async_remote_copy(
+        src_ref=src, dst_ref=dst, send_sem=send, recv_sem=recv,
+        device_id=device, device_id_type=MESH,
+    )
+
+
+def signal(device):
+    pl.semaphore_signal(
+        pltpu.get_barrier_semaphore(), inc=1, device_id=device, device_id_type=MESH
+    )
+
+
+def when(cond, fn):
+    if cond is True:
+        fn()
+    else:
+        pl.when(cond)(fn)
+
+
+def near_planes(z):
+    return (z, flip_x(z), 2 - lax.div(z, 2), 3 - 3 * lax.div(z, 2))
+
+
+def far_planes(z):
+    return (3 - 3 * lax.div(z, 2), lax.rem(2 + 3 * z, 5), 1 + lax.rem(z, 2), z)
+
+
+def span(start, size):
+    return pl.ds(pl.multiple_of(start, size), size)
+
+
+class Part:
+    def __init__(self, kind, source, target):
+        self.kind = kind
+        self.source = source
+        self.target = target
+        self.whole = kind == "small"
+
+    def own(self, m):
+        if self.kind == "rows":
+            width = self.source.shape[1] // 2
+            return self.source.at[:, span(m * width, width)]
+        return self.source
+
+    def piece(self, row, plane, core, half=None):
+        ref = self.target
+        if self.kind == "small":
+            return ref.at[plane * 4 + row, core]
+        if self.kind == "line":
+            rows = self.source.shape[0]
+            return ref.at[span(core * rows, rows), span(plane * 128, 128)]
+        if self.kind == "cols":
+            rows = self.source.shape[1] // 2
+            base = (row * 4 + plane) * 2 * rows + core * rows
+            if half is None:
+                return ref.at[span(base, rows), :]
+            return ref.at[span(base + half * (rows // 2), rows // 2), :]
+        if self.kind == "rows":
+            rows, width = self.source.shape[0], self.source.shape[1] // 2
+            cols = span(core * width, width)
+            base = (plane * 4 + row) * rows
+        elif self.kind == "chips":
+            rows, width = self.source.shape[0], self.source.shape[1] // 2
+            cols = span(core * width, width)
+            base = (row * 4 + plane) * rows
+        else:
+            rows = self.source.shape[0]
+            cols = span((row * 4 + plane) * 128, 128)
+            base = core * rows
+        if half is None:
+            return ref.at[span(base, rows), cols]
+        return ref.at[span(base + half * (rows // 2), rows // 2), cols]
+
+    def mirrored(self):
+        return self.kind in ("rows", "chips", "cols")
+
+
+class Gather:
+    Z, X, Y, DX, DY, PO, PX, PY, P0, P1, UP, DN = range(12)
+
+    def __init__(self, parts, send, recv):
+        self.parts, self.send, self.recv = parts, send, recv
+        s, z, m = place()
+        self.s, self.z, self.m = s, z, m
+        self.lines = (s, flip_x(s), flip_y(s), 3 - s)
+        self.xn, self.yn, self.pn = (self.lines[1], z, m), (self.lines[2], z, m), (s, z, 1 - m)
+        self.planes = near_planes(z)
+        self.pending = []
+
+    def own(self, k):
+        part = self.parts[k]
+        if part.kind == "chips":
+            width = part.source.shape[1] // 2
+            return part.source.at[:, span(self.m * width, width)]
+        return part.own(self.m)
+
+    def push(self, cond, k, kind, at, source, target, device, out=None):
+        out = kind if out is None else out
+        copy = lambda: remote(source, target, self.send.at[k, out, at], self.recv.at[k, kind, at], device)
+        when(cond, lambda: copy().start())
+        self.pending.append((cond, copy))
+
+    def landed(self, k, kind, at, target):
+        remote(target, target, self.send.at[k, kind, at], self.recv.at[k, kind, at], self.pn).wait_recv()
+
+    def fan(self, k, at, source):
+        target = self.parts[k].piece(self.s, at, self.m)
+        self.push(True, k, self.X, at, source, target, self.xn)
+        self.push(True, k, self.Y, at, source, target, self.yn)
+
+    def start(self):
+        z, at = self.z, self.z
+        for k, part in enumerate(self.parts):
+            source, target = self.own(k), part.piece(self.s, at, self.m)
+            self.push(z < 3, k, self.Z, at, source, target, (self.s, z + 1, self.m), self.UP)
+            self.push(z > 0, k, self.Z, at, source, target, (self.s, z - 1, self.m), self.DN)
+            self.fan(k, at, source)
+            if not part.mirrored():
+                self.push(True, k, self.PO, at, source, target, self.pn)
+
+    def along(self, step):
+        z, at = self.z, self.planes[step]
+        goal = 3 - z if step == 1 else 3 * z - 3
+        inner = jnp.logical_and(z > 0, z < 3)
+        for k, part in enumerate(self.parts):
+            target = part.piece(self.s, at, self.m)
+            self.landed(k, self.Z, at, target)
+            self.push(inner, k, self.Z, at, target, target, (self.s, goal, self.m), self.UP)
+            self.fan(k, at, target)
+            self.push(True, k, self.PO, at, target, target, self.pn)
+
+    def across(self, step):
+        at = self.planes[step]
+        for k, part in enumerate(self.parts):
+            whole = part.piece(self.lines[1], at, self.m)
+            half = whole if part.whole else part.piece(self.lines[1], at, self.m, 0)
+            self.landed(k, self.X, at, whole)
+            self.push(True, k, self.DY, at, half, half, self.yn)
+            self.push(True, k, self.PX, at, whole, whole, self.pn)
+            whole = part.piece(self.lines[2], at, self.m)
+            self.landed(k, self.Y, at, whole)
+            if not part.whole:
+                half = part.piece(self.lines[2], at, self.m, 1)
+                self.push(True, k, self.DX, at, half, half, self.xn)
+            self.push(True, k, self.PY, at, whole, whole, self.pn)
+
+    def corner(self, step):
+        at, far = self.planes[step], self.lines[3]
+        for k, part in enumerate(self.parts):
+            half = part.piece(far, at, self.m, None if part.whole else 0)
+            self.landed(k, self.DY, at, half)
+            self.push(True, k, self.P0, at, half, half, self.pn)
+            if not part.whole:
+                half = part.piece(far, at, self.m, 1)
+                self.landed(k, self.DX, at, half)
+                self.push(True, k, self.P1, at, half, half, self.pn)
+
+    def ready(self, step):
+        at, other = self.planes[step], 1 - self.m
+        for k, part in enumerate(self.parts):
+            if step > 0 or not part.mirrored():
+                self.landed(k, self.PO, at, part.piece(self.s, at, other))
+            self.landed(k, self.PX, at, part.piece(self.lines[1], at, other))
+            self.landed(k, self.PY, at, part.piece(self.lines[2], at, other))
+            self.landed(k, self.P0, at, part.piece(self.lines[3], at, other, None if part.whole else 0))
+            if not part.whole:
+                self.landed(k, self.P1, at, part.piece(self.lines[3], at, other, 1))
+
+    def finish(self):
+        for cond, copy in self.pending:
+            when(cond, lambda copy=copy: copy().wait_send())
+
+
+class Line(Gather):
+    def fan(self, k, at, source):
+        pass
+
+    def ready(self, step):
+        at = self.planes[step]
+        for k, part in enumerate(self.parts):
+            self.landed(k, self.PO, at, part.piece(self.s, at, 1 - self.m))
+
+
+class Spread(Gather):
+    def block(self, plane):
+        source = self.parts[0].source
+        rows = source.shape[1] // 2
+        return source.at[plane, span(self.m * rows, rows), :]
+
+    def start(self):
+        z = self.z
+        target = self.parts[0].piece(self.s, z, self.m)
+        for step in (1, 2, 3):
+            plane = lax.rem(z + step, 4)
+            out = (self.UP, self.DN, self.Z)[step - 1]
+            self.push(True, 0, self.Z, z, self.block(plane), target, (self.s, plane, self.m), out)
+        self.fan(0, z, self.block(z))
+
+    def along(self, step):
+        at = self.planes[step]
+        target = self.parts[0].piece(self.s, at, self.m)
+        self.landed(0, self.Z, at, target)
+        self.fan(0, at, target)
+        self.push(True, 0, self.PO, at, target, target, self.pn)
+
+
+def meet_chips():
+    s, z, m = place()
+    c = s * 4 + z
+    for step in range(1, 16):
+        j = lax.rem(c + step, 16)
+        signal((lax.div(j, 4), lax.rem(j, 4), m))
+    signal((s, z, 1 - m))
+    pl.semaphore_wait(pltpu.get_barrier_semaphore(), 16)
+
+
+def add_rows(put, sources, count, step=16):
+    def run(r, _):
+        at = span(r * step, step)
+        total = sources[0](at)
+        for source in sources[1:]:
+            total = total + source(at)
+        put(at, total)
+        return 0
+    lax.fori_loop(0, count // step, run, 0)
+
+
+def shifted(at, base, step=16):
+    return pl.ds(pl.multiple_of(at.start + base, step), step)
+
+
+class Reduce:
+    def __init__(self, pair, by_plane, src, acc, out, bufs, sems):
+        self.pair, self.by_plane, self.src, self.acc, self.out = pair, by_plane, src, acc, out
+        (self.buf0, self.bufx, self.bufy, self.bufx2, self.bufy2, self.zbuf, self.zsend, self.fin) = bufs
+        self.send, self.recv = sems
+        s, z, m = place()
+        self.s, self.z, self.m = s, z, m
+        self.xn, self.yn, self.pn = (flip_x(s), z, m), (flip_y(s), z, m), (s, z, 1 - m)
+        self.lines = (s, flip_x(s), flip_y(s), 3 - s)
+        self.rows = self.fin.shape[0]
+        self.half = self.rows // 2
+        self.width = self.fin.shape[1]
+        self.mine = span(m * self.width, self.width)
+        self.cols = self.mine if acc.shape[1] > self.width else slice(None)
+        self.other = span((1 - m) * self.width, self.width)
+        self.pending = []
+
+    def push(self, kind, at, source, target, device):
+        copy = lambda: remote(source, target, self.send.at[kind, at], self.recv.at[kind, at], device)
+        copy().start()
+        self.pending.append(copy)
+
+    def landed(self, kind, at, target):
+        remote(target, target, self.send.at[kind, at], self.recv.at[kind, at], self.pn).wait_recv()
+
+    def base(self, at, q, by_plane=None):
+        by_plane = self.by_plane if by_plane is None else by_plane
+        row = self.lines[q]
+        return (at * 4 + row if by_plane else row * 4 + at) * self.rows
+
+    def held(self, at, q):
+        return self.base(at, q, self.pair or self.by_plane)
+
+    def swap(self, at):
+        for q in (3, 1, 2, 0):
+            self.push(q, at, self.src.at[span(self.base(at, q), self.rows), self.other],
+                      self.buf0.at[at, q], self.pn)
+
+    def block(self, at, q, lo):
+        return self.acc.at[pl.ds(pl.multiple_of(self.held(at, q) + lo, self.half), self.half), self.cols]
+
+    def first(self, at):
+        for q in (3, 1, 2, 0):
+            if self.pair:
+                self.landed(q, at, self.buf0.at[at, q])
+                base = self.base(at, q)
+                held = self.held(at, q)
+
+                def put(r, v, held=held):
+                    self.acc[shifted(r, held), self.cols] = v.astype(BF)
+                add_rows(put, [
+                    lambda r, base=base: self.src[shifted(r, base), self.mine].astype(F32),
+                    lambda r, q=q: self.buf0[at, q, r].astype(F32)], self.rows)
+            if q == 3:
+                self.push(4, at, self.block(at, 3, 0), self.bufx.at[at, 1], self.xn)
+                self.push(5, at, self.block(at, 3, self.half), self.bufy.at[at, 1], self.yn)
+            if q == 1:
+                self.push(6, at, self.block(at, 1, 0), self.bufx.at[at, 0], self.xn)
+            if q == 2:
+                self.push(7, at, self.block(at, 2, self.half), self.bufy.at[at, 0], self.yn)
+
+    def local(self, at, q, lo):
+        held = self.held(at, q) + lo
+        return lambda r: self.acc[shifted(r, held), self.cols].astype(F32)
+
+    def second(self, at):
+        self.landed(4, at, self.bufx.at[at, 1])
+
+        def put_x(r, v):
+            self.bufx[at, 1, r] = v.astype(BF)
+        add_rows(put_x, [self.local(at, 2, 0), lambda r: self.bufx[at, 1, r].astype(F32)], self.half)
+        self.push(8, at, self.bufx.at[at, 1], self.bufy2.at[at], self.yn)
+        self.landed(5, at, self.bufy.at[at, 1])
+
+        def put_y(r, v):
+            self.bufy[at, 1, r] = v.astype(BF)
+        add_rows(put_y, [self.local(at, 1, self.half), lambda r: self.bufy[at, 1, r].astype(F32)], self.half)
+        self.push(9, at, self.bufy.at[at, 1], self.bufx2.at[at], self.xn)
+
+    def settle(self, at, put_low, put_high):
+        half = self.half
+        self.landed(6, at, self.bufx.at[at, 0])
+        self.landed(8, at, self.bufy2.at[at])
+        self.landed(7, at, self.bufy.at[at, 0])
+        self.landed(9, at, self.bufx2.at[at])
+        add_rows(put_low, [self.local(at, 0, 0), lambda r: self.bufx[at, 0, r].astype(F32),
+                           lambda r: self.bufy2[at, r].astype(F32)], half)
+        add_rows(put_high, [self.local(at, 0, half), lambda r: self.bufy[at, 0, r].astype(F32),
+                            lambda r: self.bufx2[at, r].astype(F32)], half)
+
+    def third(self, at, slot):
+        half = self.half
+
+        def low(r, v):
+            self.zsend[slot, r] = v.astype(BF)
+
+        def high(r, v):
+            self.zsend[slot, shifted(r, half)] = v.astype(BF)
+        self.settle(at, low, high)
+        copy = lambda: remote(self.zsend.at[slot], self.zbuf.at[self.z], self.send.at[12, slot],
+                              self.recv.at[10, self.z], (self.s, at, self.m))
+        copy().start()
+        self.pending.append(copy)
+
+    def keep(self):
+        half = self.half
+
+        def low(r, v):
+            self.fin[r] = v
+
+        def high(r, v):
+            self.fin[shifted(r, half)] = v
+        self.settle(self.z, low, high)
+
+    def close(self):
+        mine, other = self.mine, self.other
+        others = [lax.rem(self.z + step, 4) for step in (1, 2, 3)]
+        for at in others:
+            self.landed(10, at, self.zbuf.at[at])
+
+        def put(r, v):
+            self.out[r, mine] = v.astype(BF)
+        add_rows(put, [lambda r: self.fin[r]] + [
+            lambda r, at=at: self.zbuf[at, r].astype(F32) for at in others], self.rows)
+        self.push(13, 0, self.out.at[:, mine], self.out.at[:, mine], self.pn)
+
+    def landing(self):
+        self.landed(13, 0, self.out.at[:, self.other])
+
+    def finish(self):
+        for copy in self.pending:
+            copy().wait_send()
+
+
+def reduce_buffers(pair, rows, width):
+    half = rows // 2
+    return [
+        pltpu.VMEM((4, 4, rows, width) if pair else (1, 1, 16, width), BF),
+        pltpu.VMEM((4, 2, half, width), BF),
+        pltpu.VMEM((4, 2, half, width), BF),
+        pltpu.VMEM((4, half, width), BF),
+        pltpu.VMEM((4, half, width), BF),
+        pltpu.VMEM((4, rows, width), BF),
+        pltpu.VMEM((3, rows, width), BF),
+        pltpu.VMEM((rows, width), F32),
+        pltpu.SemaphoreType.DMA((14, 4)),
+        pltpu.SemaphoreType.DMA((14, 4)),
+    ]
+
+
+def experts_body(two_ref, share_ref, top_ref, gate_ref, up_ref, down_ref,
+                 back_out, prob_out, moe_out, dgate_out, dup_out, ddown_out,
+                 two_all, shares, top_all, pair_w, down_w, pull, pair_v,
+                 acts, dpair, back, prob_v, stage, dstage,
+                 buf0, bufx, bufy, bufx2, bufy2, zbuf, zsend, fin, rsend, rrecv,
+                 gsend, grecv, psend, precv, load, store, dstore):
+    s, z, m = place()
+    c = s * 4 + z
+    rows = two_ref.shape[0]
+    width = two_ref.shape[1]
+    hidden = down_w.shape[0]
+    block = 4 * rows
+    loads = [
+        pltpu.make_async_copy(top_ref, top_all, load.at[0]),
+        pltpu.make_async_copy(down_ref, down_w, load.at[1]),
+        pltpu.make_async_copy(gate_ref, pair_w.at[:, pl.ds(0, hidden)], load.at[2]),
+        pltpu.make_async_copy(up_ref, pair_w.at[:, pl.ds(hidden, hidden)], load.at[3]),
+    ]
+    for copy in loads:
+        copy.start()
+    meet_chips()
+    work = Gather([Part("rows", two_ref, two_all), Part("small", share_ref, shares)], gsend, grecv)
+    work.start()
+    two_all[span((z * 4 + s) * rows, rows), :] = two_ref[...]
+    shares[z * 4 + s, m] = share_ref[...]
+    total = Reduce(True, True, back, back, back_out,
+                   (buf0, bufx, bufy, bufx2, bufy2, zbuf, zsend, fin), (rsend, rrecv))
+    planes = work.planes
+
+    def tiles(count, size, fn):
+        def run(i, _):
+            fn(span(i * size, size))
+            return 0
+        lax.fori_loop(0, count // size, run, 0)
+
+    def pulls(i):
+        at = pl.ds(i * block, block)
+
+        def tile(cols):
+            pull[at, cols] = contract_last(top_all[at, :], down_w[cols, :])
+        tiles(hidden, 512, tile)
+
+    def enter(side, k):
+        at = span(planes[k] * block, block)
+        cols = pl.ds(side * hidden, hidden)
+        pair_v[:, cols] = jnp.dot(two_all[at, :], pair_w[:, cols], preferred_element_type=F32)
+
+    def middle(k):
+        def one(row, _):
+            slot = planes[k] * 4 + row
+            wide = jnp.broadcast_to(shares[slot, m, pl.ds(c, 1), :], (rows, rows))
+            column = jnp.transpose(wide)[:, 0:1]
+            base = span(slot * rows, rows)
+            here = span(row * rows, rows)
+            gate = pair_v[here, pl.ds(0, hidden)]
+            up = pair_v[here, pl.ds(hidden, hidden)]
+            drawn = pull[base, :]
+            sig = jax.nn.sigmoid(gate)
+            act = gate * sig * up
+            acts[base, :] = (act * column).astype(BF)
+            grad = drawn * column
+            dpair[base, pl.ds(0, hidden)] = (grad * up * sig * (1.0 + gate * (1.0 - sig))).astype(BF)
+            dpair[base, pl.ds(hidden, hidden)] = (grad * gate * sig).astype(BF)
+            prob = jnp.sum(act * drawn, axis=1, keepdims=True)
+            prob_v[slot] = jnp.transpose(jnp.broadcast_to(prob, (rows, rows)))[0:8, :]
+            return 0
+        lax.fori_loop(0, 4, one, 0)
+
+    def backs(k):
+        at = span(planes[k] * block, block)
+
+        def tile(cols):
+            back[at, cols] = contract_last(dpair[at, :], pair_w[cols, :]).astype(BF)
+        tiles(width, 1024, tile)
+        total.swap(planes[k])
+
+    def saves(i, t):
+        cols = pl.ds(t * 1024, 1024)
+        return pltpu.make_async_copy(
+            stage.at[t], moe_out.at[pl.ds(i * block, block), cols], store.at[t])
+
+    def moes(i):
+        at = pl.ds(i * block, block)
+        for t in (0, 1):
+            if i >= 1:
+                saves(i - 1, t).wait()
+            cols = pl.ds(t * 1024, 1024)
+            stage[t] = jnp.dot(acts[at, :], down_w[:, cols], preferred_element_type=F32).astype(BF)
+            saves(i, t).start()
+
+    def keep(i):
+        rows_at = span(i * 512, 512)
+        slot = lax.rem(i, 2)
+        return [
+            pltpu.make_async_copy(
+                dstage.at[slot, :, pl.ds(side * hidden, hidden)],
+                (dgate_out, dup_out)[side].at[rows_at, :],
+                dstore.at[slot, side],
+            )
+            for side in (0, 1)
+        ]
+
+    def keep_down(i):
+        return pltpu.make_async_copy(
+            dstage.at[i], ddown_out.at[:, pl.ds(i * 1024, 1024)], dstore.at[i, 2])
+
+    def grads(low, high):
+        def one(i, _):
+            def settle():
+                for copy in keep(i - 2):
+                    copy.wait()
+            pl.when(i >= 2)(settle)
+            cols = span(i * 512, 512)
+            dstage[lax.rem(i, 2)] = contract_first(two_all[:, cols], dpair[...])
+            for copy in keep(i):
+                copy.start()
+            return 0
+        lax.fori_loop(low, high, one, 0)
+
+    def downs():
+        for i in (2, 3):
+            for copy in keep(i):
+                copy.wait()
+        for i in (0, 1):
+            dstage[i] = contract_first(acts[...], top_all[:, pl.ds(i * 1024, 1024)])
+            keep_down(i).start()
+
+    loads[0].wait()
+    loads[1].wait()
+    pulls(0)
+    work.along(1)
+    work.across(0)
+    pulls(1)
+    work.along(2)
+    work.across(1)
+    pulls(2)
+    work.along(3)
+    work.corner(0)
+    pulls(3)
+    work.across(2)
+    loads[2].wait()
+    loads[3].wait()
+    work.ready(0)
+    enter(0, 0)
+    work.corner(1)
+    enter(1, 0)
+    work.across(3)
+    middle(0)
+    work.corner(2)
+    backs(0)
+    work.ready(1)
+    enter(0, 1)
+    work.corner(3)
+    enter(1, 1)
+    total.first(planes[0])
+    middle(1)
+    backs(1)
+    total.second(planes[0])
+    work.ready(2)
+    enter(0, 2)
+    total.first(planes[1])
+    enter(1, 2)
+    middle(2)
+    backs(2)
+    total.second(planes[1])
+    work.ready(3)
+    enter(0, 3)
+    total.first(planes[2])
+    enter(1, 3)
+    middle(3)
+
+    def dev(j):
+        return (lax.div(j, 4), lax.rem(j, 4), m)
+
+    def send_prob(step):
+        j = lax.rem(c + step, 16)
+        slot = lax.rem(j, 4) * 4 + lax.div(j, 4)
+        return remote(prob_v.at[slot], prob_out.at[m, c], psend.at[step], precv.at[step], dev(j))
+    for step in range(1, 16):
+        send_prob(step).start()
+    prob_out[m, c] = prob_v[z * 4 + s]
+    backs(3)
+    total.second(planes[2])
+    moes(0)
+    total.first(planes[3])
+    total.keep()
+    moes(1)
+    total.third(planes[1], 0)
+    moes(2)
+    total.second(planes[3])
+    total.third(planes[2], 1)
+    moes(3)
+    grads(0, 1)
+    total.third(planes[3], 2)
+    grads(1, 3)
+    for step in range(1, 16):
+        j = lax.rem(c + 16 - step, 16)
+        target = prob_out.at[m, j]
+        remote(target, target, psend.at[step], precv.at[step], dev(j)).wait_recv()
+    pair = remote(prob_out.at[m], prob_out.at[m], psend.at[0], precv.at[0], (s, z, 1 - m))
+    pair.start()
+    grads(3, 4)
+    downs()
+    total.close()
+    for i in (0, 1):
+        keep_down(i).wait()
+    for t in (0, 1):
+        saves(3, t).wait()
+    total.landing()
+    other = prob_out.at[1 - m]
+    remote(other, other, psend.at[0], precv.at[0], (s, z, 1 - m)).wait_recv()
+    pair.wait_send()
+    for step in range(1, 16):
+        send_prob(step).wait_send()
+    work.finish()
+    total.finish()
+
+
+def experts(ident, two, share, top, gate, up, down):
+    rows, width = two.shape
+    hidden = gate.shape[1]
+    every = 16 * rows
+    block = 4 * rows
+    vmem = pl.BlockSpec(memory_space=pltpu.VMEM)
+    hbm = pl.BlockSpec(memory_space=pl.ANY)
+    return pl.pallas_call(
+        experts_body,
+        out_shape=(
+            jax.ShapeDtypeStruct((rows, width), BF),
+            jax.ShapeDtypeStruct((2, 16, 8, rows), F32),
+            jax.ShapeDtypeStruct((every, width), BF),
+            jax.ShapeDtypeStruct((width, hidden), F32),
+            jax.ShapeDtypeStruct((width, hidden), F32),
+            jax.ShapeDtypeStruct((hidden, width), F32),
+        ),
+        in_specs=[vmem, vmem, hbm, hbm, hbm, hbm],
+        out_specs=(vmem, vmem, hbm, hbm, hbm, hbm),
+        scratch_shapes=[
+            pltpu.VMEM((every, width), BF),
+            pltpu.VMEM((16, 2) + share.shape, F32),
+            pltpu.VMEM((every, width), BF),
+            pltpu.VMEM((width, 2 * hidden), BF),
+            pltpu.VMEM((hidden, width), BF),
+            pltpu.VMEM((every, hidden), F32),
+            pltpu.VMEM((block, 2 * hidden), F32),
+            pltpu.VMEM((every, hidden), BF),
+            pltpu.VMEM((every, 2 * hidden), BF),
+            pltpu.VMEM((every, width), BF),
+            pltpu.VMEM((16, 8, rows), F32),
+            pltpu.VMEM((2, block, 1024), BF),
+            pltpu.VMEM((2, 512, 2 * hidden), F32),
+        ]
+        + reduce_buffers(True, rows, width // 2)
+        + [
+            pltpu.SemaphoreType.DMA((2, 12, 4)),
+            pltpu.SemaphoreType.DMA((2, 12, 4)),
+            pltpu.SemaphoreType.DMA((16,)),
+            pltpu.SemaphoreType.DMA((16,)),
+            pltpu.SemaphoreType.DMA((4,)),
+            pltpu.SemaphoreType.DMA((2,)),
+            pltpu.SemaphoreType.DMA((2, 3)),
+        ],
+        compiler_params=pltpu.CompilerParams(collective_id=ident, has_side_effects=True,
+                                             vmem_limit_bytes=66900000),
+        name="experts_%d" % ident,
+    )(two, share, top, gate, up, down)
+
+
+class Hand:
+    def __init__(self, source, target, send, recv):
+        s, z, m = place()
+        self.c, self.m, self.pn = s * 4 + z, m, (s, z, 1 - m)
+        self.source, self.target, self.send, self.recv = source, target, send, recv
+
+    def dev(self, j):
+        return (lax.div(j, 4), lax.rem(j, 4), self.m)
+
+    def copy(self, step):
+        j = lax.rem(self.c + step, 16)
+        return remote(self.source(j), self.target(self.c), self.send.at[step], self.recv.at[step], self.dev(j))
+
+    def start(self):
+        for step in range(1, 16):
+            self.copy(step).start()
+
+    def collect(self):
+        for step in range(1, 16):
+            j = lax.rem(self.c + 16 - step, 16)
+            remote(self.target(j), self.target(j), self.send.at[step], self.recv.at[step], self.pn).wait_recv()
+
+    def finish(self):
+        for step in range(1, 16):
+            self.copy(step).wait_send()
+
+
+class Chips:
+    def __init__(self, source, target, send, recv, fsend, frecv, local):
+        s, z, m = place()
+        self.c, self.m, self.pn = s * 4 + z, m, (s, z, 1 - m)
+        self.first = lax.div(self.c, 8) == m
+        self.source, self.target = source, target
+        self.send, self.recv, self.fsend, self.frecv, self.local = send, recv, fsend, frecv, local
+
+    def copy(self, i):
+        j = 8 * self.m + i
+        return remote(self.source(i), self.target.at[self.c], self.send.at[i], self.recv.at[self.c],
+                      (lax.div(j, 4), lax.rem(j, 4), self.m))
+
+    def mine(self):
+        return pltpu.make_async_copy(
+            self.source(lax.rem(self.c, 8)), self.target.at[self.c], self.local.at[0])
+
+    def each(self, fn):
+        for step in range(8):
+            i = lax.rem(self.c + 1 + step, 8)
+            pl.when(8 * self.m + i != self.c)(lambda i=i: fn(self.copy(i)))
+
+    def start(self):
+        self.each(lambda copy: copy.start())
+        pl.when(self.first)(lambda: self.mine().start())
+
+    def forward(self, j):
+        return remote(self.target.at[j], self.target.at[j], self.fsend.at[j], self.frecv.at[j], self.pn)
+
+    def collect(self):
+        def take():
+            self.mine().wait()
+            self.forward(self.c).start()
+            for step in range(1, 16):
+                j = lax.rem(self.c + 16 - step, 16)
+                remote(self.target.at[j], self.target.at[j], self.send.at[0], self.recv.at[j],
+                       self.pn).wait_recv()
+                self.forward(j).start()
+        pl.when(self.first)(take)
+
+    def follow(self):
+        def wait():
+            for j in range(16):
+                self.forward(j).wait_recv()
+        pl.when(jnp.logical_not(self.first))(wait)
+
+    def finish(self):
+        def wait():
+            for j in range(16):
+                self.forward(j).wait_send()
+        pl.when(self.first)(wait)
+        self.each(lambda copy: copy.wait_send())
+
+
+def chips_semaphores():
+    return [pltpu.SemaphoreType.DMA((8,))] + [pltpu.SemaphoreType.DMA((16,))] * 3 + [
+        pltpu.SemaphoreType.DMA((1,))]
+
+
+def front_body(tok_ref, one_ref, second_ref, place_ref, router_ref, qg_ref, kg_ref, routes_ref,
+               qw_ref, kw_ref, vw_ref, wo_ref, cot_ref, freq_ref,
+               n1_out, wo_out, cot_out, w3, info, raw, rows3, squares, mixed, lse, trig, own_mixed,
+               hidden, two, probs_out, chosen_out, share_out, heads_out, gain_out,
+               info_ref, packed_ref, n1_own, n1_all, wo_all, wide_mixed, gathered, sums, line,
+               nsend, nrecv, osend, orecv, csend, crecv,
+               isend, irecv, qsend, qrecv, pairs, *chips_sems):
+    s, z, m = place()
+    c = s * 4 + z
+    pn = (s, z, 1 - m)
+    rows, width = tok_ref.shape
+    dim = 128
+    planes = near_planes(z)
+    lane = lax.broadcasted_iota(jnp.int32, (rows, dim), 1)
+    info_ref[...] = jnp.zeros_like(info_ref)
+    info_ref[0:1, :] = one_ref[...].astype(F32)
+    info_ref[1:2, :] = second_ref[...].astype(F32)
+    info_ref[2:3, :] = place_ref[...].astype(F32)
+    info_ref[4:20, :] = router_ref[...].astype(F32)
+    info_ref[24:32, 0:8] = qg_ref[...].astype(F32)
+    info_ref[32:40, 0:8] = kg_ref[...].astype(F32)
+    for i in range(8):
+        for n, ref in enumerate((qw_ref, kw_ref, vw_ref)):
+            packed_ref[i, :, pl.ds(n * dim, dim)] = ref[:, pl.ds(i * dim, dim)]
+    meet_chips()
+    hand = Hand(lambda j: info_ref, lambda j: info.at[m, j], isend, irecv)
+    hand.start()
+    weights = Chips(lambda i: packed_ref.at[i], w3, *chips_sems[:5])
+    weights.start()
+    info[m, c] = info_ref[...]
+
+    def square_sum(r, _):
+        at = span(r * 16, 16)
+        x = tok_ref[at, :].astype(F32)
+        mean = jnp.sum(x * x, axis=1, keepdims=True) / width
+        line[at, :] = jnp.broadcast_to(lax.rsqrt(mean + eps), (16, dim))
+        return 0
+    lax.fori_loop(0, rows // 16, square_sum, 0)
+    hand.collect()
+    swap = remote(info.at[m], info.at[m], pairs.at[0], pairs.at[1], pn)
+    swap.start()
+
+    def normalize(j, _):
+        at = span(j * dim, dim)
+        n1_own[:, at] = (tok_ref[:, at].astype(F32) * line[...] * info[m, j, 0:1, :]).astype(BF)
+        return 0
+    lax.fori_loop(0, 16, normalize, 0)
+    first = Gather([Part("rows", n1_own, n1_all)], nsend, nrecv)
+    first.start()
+    n1_all[span((z * 4 + s) * rows, rows), :] = n1_own[...]
+
+    def tables(b, _):
+        spot = jnp.broadcast_to(info[m, 8 * m + b, 2:3, :], (rows, dim))
+        angle = jnp.transpose(spot) * freq_ref[0:1, :]
+        trig[0, b] = jnp.cos(angle)
+        trig[1, b] = jnp.where(lane < dim // 2, -jnp.sin(angle), jnp.sin(angle))
+        return 0
+    lax.fori_loop(0, 8, tables, 0)
+    other = info.at[1 - m]
+    remote(other, other, pairs.at[0], pairs.at[1], pn).wait_recv()
+
+    first.along(1)
+    first.across(0)
+    weights.collect()
+    first.along(2)
+    first.across(1)
+    first.along(3)
+    first.corner(0)
+    weights.follow()
+    first.across(2)
+    first.ready(0)
+
+    def project(k):
+        value = jnp.dot(n1_all[span((planes[k] * 4 + 2 * m) * rows, 2 * rows), :],
+                        w3[...].reshape(width, 3 * dim), preferred_element_type=F32)
+        for e in (0, 1):
+            part = value[e * rows : (e + 1) * rows, :]
+            base = span((e * 4 + planes[k]) * rows, rows)
+            raw[base, :] = part[:, : 2 * dim]
+            rows3[base, pl.ds(2 * dim, dim)] = part[:, 2 * dim :].astype(BF)
+    project(0)
+    first.corner(1)
+    first.across(3)
+    outer = Gather([Part("heads", wo_ref, wo_all)], osend, orecv)
+    outer.start()
+    first.ready(1)
+    project(1)
+    first.corner(2)
+    first.ready(2)
+    project(2)
+    first.corner(3)
+    first.ready(3)
+    project(3)
+
+    def norms(b, total):
+        at = span(b * rows, rows)
+        q = raw[at, pl.ds(0, dim)]
+        k = raw[at, pl.ds(dim, dim)]
+        total = jnp.where(lane == b, jnp.sum(q * q, axis=1, keepdims=True), total)
+        return jnp.where(lane == b + 8, jnp.sum(k * k, axis=1, keepdims=True), total)
+    total = lax.fori_loop(0, 8, norms, jnp.zeros((rows, dim), F32))
+    sums[...] = jnp.transpose(total)[0:16, :]
+    share = Hand(lambda j: sums, lambda j: gathered.at[j], qsend, qrecv)
+    share.start()
+    gathered[c] = sums[...]
+    save_n1 = pltpu.make_async_copy(n1_all, n1_out, pairs.at[2])
+    save_n1.start()
+    wo_own = pltpu.make_async_copy(wo_ref, outer.parts[0].piece(s, z, m), pairs.at[3])
+    wo_own.start()
+    share.collect()
+
+    def add_up(j, acc):
+        return acc + gathered[j]
+    summed = lax.fori_loop(1, 16, add_up, gathered[0])
+    squares[...] = summed
+    wide = jnp.concatenate([lax.rsqrt(summed / width + eps), jnp.zeros((rows - 16, dim), F32)], axis=0)
+    line[...] = jnp.transpose(wide)
+    outer.along(1)
+
+    def head_gain(which):
+        total = jnp.zeros((8, dim), F32)
+        lane8 = lax.broadcasted_iota(jnp.int32, (8, dim), 1)
+        for j in range(16):
+            row = info[lax.div(c, 8), j, pl.ds(24 + 8 * which + lax.rem(c, 8), 1), :]
+            moved = pltpu.roll(jnp.broadcast_to(row, (8, dim)), 8 * j, 1)
+            total = jnp.where(lax.div(lane8, 8) == j, moved, total)
+        return total[0:1, :]
+    gains = (head_gain(0), head_gain(1))
+    heads_out[...] = jnp.concatenate([gains[0], gains[1], jnp.zeros((6, dim), F32)], axis=0)
+
+    def turn(b, _):
+        at = span(b * rows, rows)
+        for which, factor in ((0, dim ** (-0.5)), (1, 1.0)):
+            pick = jnp.where(lane == b + 8 * which, line[...], 0.0)
+            inverse = jnp.sum(pick, axis=1, keepdims=True)
+            value = raw[at, pl.ds(which * dim, dim)] * inverse * gains[which]
+            value = value * trig[0, b] + pltpu.roll(value, dim // 2, 1) * trig[1, b]
+            rows3[at, pl.ds(which * dim, dim)] = (value * factor).astype(BF)
+        return 0
+    lax.fori_loop(0, 8, turn, 0)
+    outer.across(0)
+    outer.along(2)
+
+    def attend(b, _):
+        seq = span(lax.div(b, 4) * 4 * rows, 4 * rows)
+        at = span(b * rows, rows)
+        scores = contract_last(rows3[at, pl.ds(0, dim)], rows3[seq, pl.ds(dim, dim)])
+        here = lax.broadcasted_iota(jnp.int32, scores.shape, 0) + lax.rem(b, 4) * rows
+        allowed = lax.broadcasted_iota(jnp.int32, scores.shape, 1) <= here
+        scores = jnp.where(allowed, scores, neg_big)
+        top = jnp.max(scores, axis=1, keepdims=True)
+        weight = jnp.where(allowed, jnp.exp(scores - top), 0.0)
+        count = jnp.sum(weight, axis=1, keepdims=True)
+        value = jnp.dot(weight.astype(BF), rows3[seq, pl.ds(2 * dim, dim)], preferred_element_type=F32)
+        mixed[b] = (value / count).astype(BF)
+        lse[b] = jnp.transpose(jnp.broadcast_to(top + jnp.log(count), (rows, dim)))[0:8, :]
+        return 0
+    lax.fori_loop(0, 8, attend, 0)
+    back = Chips(lambda i: mixed.at[i], own_mixed, *chips_sems[5:])
+    back.start()
+    outer.across(1)
+    outer.along(3)
+    outer.corner(0)
+    outer.across(2)
+    back.collect()
+    outer.corner(1)
+    outer.across(3)
+    cots = Gather([Part("rows", cot_ref, cot_out)], csend, crecv)
+    cots.start()
+    cot_own = pltpu.make_async_copy(cot_ref, cot_out.at[span((z * 4 + s) * rows, rows)], pairs.at[4])
+    cot_own.start()
+    outer.corner(2)
+    back.follow()
+    outer.corner(3)
+    wo_own.wait()
+    for step in range(4):
+        outer.ready(step)
+    save_wo = pltpu.make_async_copy(wo_all, wo_out, pairs.at[5])
+    save_wo.start()
+    cots.along(1)
+    cots.across(0)
+    for j in range(16):
+        wide_mixed[:, pl.ds(j * dim, dim)] = own_mixed[j]
+
+    def outward(j, _):
+        at = span(j * 512, 512)
+        hidden[:, at] = tok_ref[:, at].astype(F32) + jnp.dot(
+            wide_mixed[...], wo_all[:, at], preferred_element_type=F32)
+        return 0
+    lax.fori_loop(0, 4, outward, 0)
+    cots.along(2)
+    cots.across(1)
+
+    def square_two(r, _):
+        at = span(r * 8, 8)
+        x = hidden[at, :]
+        mean = jnp.sum(x * x, axis=1, keepdims=True) / width
+        line[at, :] = jnp.broadcast_to(lax.rsqrt(mean + eps), (8, dim))
+        return 0
+    lax.fori_loop(0, rows // 8, square_two, 0)
+
+    def normalize_two(j, _):
+        at = span(j * dim, dim)
+        two[:, at] = (hidden[:, at] * line[...] * info[m, j, 1:2, :]).astype(BF)
+        return 0
+    lax.fori_loop(0, 16, normalize_two, 0)
+    logits = jnp.zeros((16, rows), F32)
+    for j in range(16):
+        logits = logits + contract_last(info[m, j, 4:20, :].astype(BF), two[:, pl.ds(j * dim, dim)])
+        gain_out[0:1, pl.ds(j * dim, dim)] = info[m, j, 0:1, :]
+        gain_out[1:2, pl.ds(j * dim, dim)] = info[m, j, 1:2, :]
+    gain_out[2:8, :] = jnp.zeros((6, width), F32)
+    logits = jnp.exp(logits - jnp.max(logits, axis=0, keepdims=True))
+    probs = logits / jnp.sum(logits, axis=0, keepdims=True)
+    picks = jnp.transpose(jnp.concatenate(
+        [routes_ref[...].astype(F32), jnp.full((rows, dim - 8), -1.0, F32)], axis=1))
+    row16 = lax.broadcasted_iota(jnp.int32, (16, rows), 0).astype(F32)
+    chosen = jnp.zeros((16, rows), F32)
+    for k in range(8):
+        chosen = jnp.where(row16 == picks[k : k + 1, :], 1.0, chosen)
+    probs_out[...] = probs
+    chosen_out[...] = chosen
+    share_out[...] = probs * chosen
+    cots.along(3)
+    cots.corner(0)
+    cots.across(2)
+    cots.corner(1)
+    cots.across(3)
+    cots.corner(2)
+    cots.corner(3)
+    for step in range(4):
+        cots.ready(step)
+    for copy in (save_n1, save_wo, cot_own):
+        copy.wait()
+    swap.wait_send()
+    for work in (hand, weights, share, back, first, outer, cots):
+        work.finish()
+
+
+def front(ident, *arrays):
+    rows, width = arrays[0].shape
+    every = 16 * rows
+    mine = every // 2
+    vmem = pl.BlockSpec(memory_space=pltpu.VMEM)
+    hbm = pl.BlockSpec(memory_space=pl.ANY)
+
+    def shape(*sizes, dtype=F32):
+        return jax.ShapeDtypeStruct(sizes, dtype)
+    return pl.pallas_call(
+        front_body,
+        out_shape=(
+            shape(every, width, dtype=BF),
+            shape(every, width, dtype=BF),
+            shape(every, width, dtype=BF),
+            shape(16, rows, 384, dtype=BF),
+            shape(2, 16, 40, 128),
+            shape(mine, 256),
+            shape(mine, 384, dtype=BF),
+            shape(16, 128),
+            shape(8, rows, 128, dtype=BF),
+            shape(8, 8, rows),
+            shape(2, 8, rows, 128),
+            shape(16, rows, 128, dtype=BF),
+            shape(rows, width),
+            shape(rows, width, dtype=BF),
+            shape(16, rows),
+            shape(16, rows),
+            shape(16, rows),
+            shape(8, 128),
+            shape(8, width),
+        ),
+        in_specs=[vmem] * 14,
+        out_specs=(hbm, hbm, hbm) + (vmem,) * 16,
+        scratch_shapes=[
+            pltpu.VMEM((40, 128), F32),
+            pltpu.VMEM((8, rows, 384), BF),
+            pltpu.VMEM((rows, width), BF),
+            pltpu.VMEM((every, width), BF),
+            pltpu.VMEM((every, width), BF),
+            pltpu.VMEM((rows, width), BF),
+            pltpu.VMEM((16, 16, 128), F32),
+            pltpu.VMEM((16, 128), F32),
+            pltpu.VMEM((rows, 128), F32),
+        ]
+        + [pltpu.SemaphoreType.DMA((1, 12, 4))] * 6
+        + [pltpu.SemaphoreType.DMA((16,))] * 4
+        + [pltpu.SemaphoreType.DMA((6,))]
+        + chips_semaphores() * 2,
+        compiler_params=pltpu.CompilerParams(collective_id=ident, has_side_effects=True,
+                                             vmem_limit_bytes=56 << 20),
+        name="front_%d" % ident,
+    )(*arrays)
+
+
+class Cores:
+    def __init__(self, source, target, send, recv, local):
+        s, z, m = place()
+        self.c, self.m = s * 4 + z, m
+        self.high, self.low = lax.div(self.c, 8), lax.rem(self.c, 8)
+        self.same = self.high == m
+        self.source, self.target, self.send, self.recv, self.local = source, target, send, recv, local
+
+    def dev(self, i):
+        j = 8 * self.m + i
+        return (lax.div(j, 4), lax.rem(j, 4), self.high)
+
+    def away(self, i):
+        return jnp.logical_not(jnp.logical_and(self.same, self.low == i))
+
+    def copy(self, i):
+        return remote(self.source.at[i], self.target.at[self.low], self.send.at[i],
+                      self.recv.at[self.low], self.dev(i))
+
+    def mine(self):
+        return pltpu.make_async_copy(self.source.at[self.low], self.target.at[self.low], self.local.at[0])
+
+    def start(self, low=0, high=8):
+        for i in range(low, high):
+            pl.when(self.away(i))(lambda i=i: self.copy(i).start())
+
+            def keep():
+                self.mine().start()
+            pl.when(jnp.logical_not(self.away(i)))(keep)
+
+    def collect(self):
+        for i in range(8):
+            pl.when(self.away(i))(lambda i=i: remote(
+                self.target.at[i], self.target.at[i], self.send.at[0], self.recv.at[i],
+                self.dev(i)).wait_recv())
+        pl.when(self.same)(lambda: self.mine().wait())
+
+    def finish(self):
+        for i in range(8):
+            pl.when(self.away(i))(lambda i=i: self.copy(i).wait_send())
+
+
+def cores_semaphores():
+    return [pltpu.SemaphoreType.DMA((8,))] * 2 + [pltpu.SemaphoreType.DMA((1,))]
+
+
+def meet_all():
+    s, z, m = place()
+    c = s * 4 + z
+    high = lax.div(c, 8)
+    for step in range(1, 16):
+        j = lax.rem(c + step, 16)
+        signal((lax.div(j, 4), lax.rem(j, 4), m))
+    signal((s, z, 1 - m))
+
+    def cross():
+        for i in range(8):
+            j = 8 * m + i
+            signal((lax.div(j, 4), lax.rem(j, 4), high))
+        pl.semaphore_wait(pltpu.get_barrier_semaphore(), 24)
+    pl.when(high != m)(cross)
+    pl.when(high == m)(lambda: pl.semaphore_wait(pltpu.get_barrier_semaphore(), 16))
+
+
+def rear_body(back_ref, prob_ref, probs_ref, chosen_ref, two_ref, out_ref, cot_ref, info,
+              mixed_ref, rows3, raw, squares, lse, trig, gains, w3, tok_ref, gain_ref,
+              wo_ref, n1_ref, moe_ref,
+              gn_out, moe_out, q_out, k_out, v_out, out_grad, tok_out, tail_out,
+              got, ga_ref, hidden_ref, wo_half, n1_half, moe, gn_part, mixed_line, ga_blocks, ga_plane, gm_send, gm, wsend, backs,
+              dq, dk, dv, sums, gathered, line, dots, tail, out_mine, out_all,
+              a0, a1, a2, a3, a4, a5, a6, a7, asend, arecv,
+              b0, b1, b2, b3, b4, b5, b6, b7, bsend, brecv,
+              msend, mrecv, csend, crecv, hsend, hrecv, tsend, trecv, psend, precv, osend, orecv, load, *rest):
+    s, z, m = place()
+    c = s * 4 + z
+    pn = (s, z, 1 - m)
+    rows, width = tok_ref.shape
+    cut = width // 2
+    dim = 128
+    factor = dim ** (-0.5)
+    loads = [
+        pltpu.make_async_copy(wo_ref.at[span(m * cut, cut), :], wo_half, load.at[0]),
+        pltpu.make_async_copy(moe_ref, moe, load.at[1]),
+        pltpu.make_async_copy(n1_ref.at[:, span(m * cut, cut)], n1_half, load.at[2]),
+        pltpu.make_async_copy(mixed_ref, mixed_line.at[span(m * cut, cut), span(z * dim, dim)], load.at[3]),
+    ]
+    for copy in loads:
+        copy.start()
+    prob = jnp.concatenate(
+        [prob_ref[0, j, 0:1, :] + prob_ref[1, j, 0:1, :] for j in range(16)], axis=0)
+    prob = prob * chosen_ref[...]
+    probs = probs_ref[...]
+    logits = (probs * (prob - jnp.sum(probs * prob, axis=0, keepdims=True))).astype(BF)
+    tail[...] = jnp.zeros_like(tail)
+    for j in range(16):
+        at = pl.ds(j * dim, dim)
+        tail[j, 3:19, :] = jnp.dot(logits, two_ref[:, at], preferred_element_type=F32)
+        hidden_ref[:, at] = back_ref[:, at].astype(F32) + contract_first(
+            logits, info[m, j, 4:20, :].astype(BF))
+
+    def second_norm(r, acc):
+        at = span(r * 16, 16)
+        x = out_ref[at, :]
+        grad = hidden_ref[at, :]
+        inverse = lax.rsqrt(jnp.sum(x * x, axis=1, keepdims=True) / width + eps)
+        scaled = grad * gain_ref[1:2, :]
+        dot = jnp.sum(x * scaled, axis=1, keepdims=True) / width
+        value = cot_ref[at, :].astype(F32) + (
+            inverse * scaled - x * (inverse * inverse * inverse * dot))
+        hidden_ref[at, :] = value
+        ga_ref[at, :] = value.astype(BF)
+        part = grad * x * inverse
+        return acc + part[0:8] + part[8:16]
+    acc = lax.fori_loop(0, rows // 16, second_norm, jnp.zeros((8, width), F32))
+    acc = jnp.sum(acc, axis=0, keepdims=True)
+    for j in range(16):
+        tail[j, 1:2, :] = acc[:, j * dim : (j + 1) * dim]
+    meet_all()
+    lane = lax.broadcasted_iota(jnp.int32, (rows, dim), 1)
+    order = far_planes(z)
+    give = Cores(gm_send, gm, *rest[:3])
+    loads[0].wait()
+    for t in range(2):
+        value = contract_last(ga_ref[...], wo_half[pl.ds(t * 512, 512), :]).astype(BF)
+        for i in range(4):
+            gm_send[t * 4 + i] = value[:, i * dim : (i + 1) * dim]
+        give.start(t * 4, t * 4 + 4)
+    strip = Line([Part("line", mixed_ref, mixed_line)], msend, mrecv)
+    spread = Spread([Part("cols", ga_blocks, ga_plane)], csend, crecv)
+    loads[1].wait()
+    outer = Reduce(True, True, moe, moe, moe_out, (a0, a1, a2, a3, a4, a5, a6, a7), (asend, arecv))
+    inner = Reduce(False, True, gn_part, gn_part, gn_out, (b0, b1, b2, b3, b4, b5, b6, b7), (bsend, brecv))
+    for at in order:
+        outer.swap(at)
+
+    wide = jnp.concatenate(
+        [lax.rsqrt(squares[...] / width + eps), jnp.zeros((rows - 16, dim), F32)], axis=0)
+    line[...] = jnp.transpose(wide)
+    dk[...] = jnp.zeros_like(dk)
+    dv[...] = jnp.zeros_like(dv)
+    outer.first(order[0])
+    outer.first(order[1])
+    give.collect()
+    outer.first(order[2])
+    outer.first(order[3])
+
+    def attend(b, _):
+        seq = span(lax.div(b, 4) * 4 * rows, 4 * rows)
+        at = span(b * rows, rows)
+        query = rows3[at, pl.ds(0, dim)]
+        key = rows3[seq, pl.ds(dim, dim)]
+        value = rows3[seq, pl.ds(2 * dim, dim)]
+        grad = gm[b]
+        top = jnp.transpose(jnp.broadcast_to(lse[b, 0:1, :], (rows, dim)))[:, 0:1]
+        delta = jnp.sum(grad.astype(F32) * mixed_ref[at, :].astype(F32), axis=1, keepdims=True)
+        scores = contract_last(query, key)
+        here = lax.broadcasted_iota(jnp.int32, scores.shape, 0) + lax.rem(b, 4) * rows
+        allowed = lax.broadcasted_iota(jnp.int32, scores.shape, 1) <= here
+        prob = jnp.where(allowed, jnp.exp(jnp.where(allowed, scores, neg_big) - top), 0.0)
+        back = (prob * (contract_last(grad, value) - delta)).astype(BF)
+        dv[seq, :] += contract_first(prob.astype(BF), grad)
+        dk[seq, :] += contract_first(back, query)
+        dq[at, :] = jnp.dot(back, key, preferred_element_type=F32) * factor
+        return 0
+    lax.fori_loop(0, 4, attend, 0)
+    outer.second(order[0])
+    outer.second(order[1])
+    lax.fori_loop(4, 8, attend, 0)
+
+    def column(source, r):
+        return jnp.sum(jnp.where(lane == r, source, 0.0), axis=1, keepdims=True)
+
+    def unturn(b, carry):
+        total, gain_q, gain_k = carry
+        at = span(b * rows, rows)
+        out = []
+        for which, grads in ((0, dq), (1, dk)):
+            value = grads[at, :]
+            value = value * trig[0, b] + pltpu.roll(value * trig[1, b], dim // 2, 1)
+            plain = raw[at, pl.ds(which * dim, dim)]
+            unit = plain * column(line[...], b + 8 * which)
+            out.append(jnp.sum(value * unit, axis=0, keepdims=True))
+            value = value * gains[which : which + 1, :]
+            grads[at, :] = value
+            dot = jnp.sum(plain * value, axis=1, keepdims=True)
+            total = jnp.where(lane == b + 8 * which, dot, total)
+        return total, gain_q + out[0], gain_k + out[1]
+    zero = jnp.zeros((1, dim), F32)
+    total, gain_q, gain_k = lax.fori_loop(0, 8, unturn, (jnp.zeros((rows, dim), F32), zero, zero))
+    for j in range(16):
+        tail[j, 2:3, :] = gain_q
+        tail[j, 19:20, :] = gain_k
+    sums[...] = jnp.transpose(total)[0:16, :]
+    hand = Hand(lambda j: sums, lambda j: gathered.at[j], hsend, hrecv)
+    hand.start()
+    gathered[c] = sums[...]
+    strip.start()
+    for p in range(4):
+        for q in range(4):
+            ga_blocks[p, :, pl.ds(q * dim, dim)] = ga_ref[:, pl.ds((q * 4 + p) * dim, dim)]
+    spread.start()
+    ga_plane[span(c * rows, rows), :] = ga_blocks[z]
+    outer.second(order[2])
+    outer.third(order[0], 0)
+    outer.second(order[3])
+    outer.third(order[1], 1)
+    hand.collect()
+    summed = lax.fori_loop(1, 16, lambda j, acc: acc + gathered[j], gathered[0])
+    dots[...] = jnp.transpose(jnp.concatenate([summed, jnp.zeros((rows - 16, dim), F32)], axis=0))
+
+    def finish_rows(b, _):
+        at = span(b * rows, rows)
+        base = span((lax.rem(b, 4) * 4 + 2 * m + lax.div(b, 4)) * rows, rows)
+        for which, grads in ((0, dq), (1, dk)):
+            inverse = column(line[...], b + 8 * which)
+            dot = column(dots[...], b + 8 * which)
+            value = inverse * grads[at, :] - raw[at, pl.ds(which * dim, dim)] * (
+                inverse * inverse * inverse * dot / width)
+            backs[base, pl.ds(which * dim, dim)] = value.astype(BF)
+        backs[base, pl.ds(2 * dim, dim)] = dv[at, :].astype(BF)
+        return 0
+    lax.fori_loop(0, 8, finish_rows, 0)
+
+    def pair(at, core):
+        part = backs.at[span((at * 4 + 2 * core) * rows, 2 * rows), :]
+        return remote(part, part, psend.at[at], precv.at[at], pn)
+    for at in range(4):
+        pair(at, m).start()
+    outer.third(order[2], 2)
+    for at in range(4):
+        pair(at, 1 - m).wait_recv()
+    for at in order:
+        here = span(at * 4 * rows, 4 * rows)
+        gn_part[here, :] = contract_last(
+            backs[here, :], w3[span(m * 8, 8)].reshape(cut, 3 * dim)).astype(BF)
+        inner.first(at)
+    outer.keep()
+    strip.along(1)
+    spread.along(1)
+    loads[2].wait()
+
+    def weight_tile(t):
+        value = contract_first(n1_half[:, pl.ds(t * 256, 256)], backs[...]).astype(BF)
+        wsend[2 * t] = value[:rows]
+        wsend[2 * t + 1] = value[rows:]
+    weight_tile(0)
+    weight_tile(1)
+    inner.second(order[0])
+    weight_tile(2)
+    inner.third(order[0], 0)
+    inner.second(order[1])
+    weight_tile(3)
+    outer.close()
+    weights = Cores(wsend, got, *rest[3:6])
+    weights.start()
+    strip.along(2)
+    spread.along(2)
+    spread.across(0)
+    inner.third(order[1], 1)
+    inner.second(order[2])
+    inner.third(order[2], 2)
+    inner.second(order[3])
+    inner.keep()
+    strip.along(3)
+    spread.along(3)
+    spread.across(1)
+    spread.corner(0)
+    inner.close()
+    inner.landing()
+
+    def last(r, acc):
+        at = span(r * 16, 16)
+        x = tok_ref[at, :].astype(F32)
+        grad = gn_out[at, :].astype(F32)
+        inverse = lax.rsqrt(jnp.sum(x * x, axis=1, keepdims=True) / width + eps)
+        scaled = grad * gain_ref[0:1, :]
+        dot = jnp.sum(x * scaled, axis=1, keepdims=True) / width
+        tok_out[at, :] = hidden_ref[at, :] + inverse * scaled - x * (inverse * inverse * inverse * dot)
+        part = grad * x * inverse
+        return acc + part[0:8] + part[8:16]
+    acc = lax.fori_loop(0, rows // 16, last, jnp.zeros((8, width), F32))
+    acc = jnp.sum(acc, axis=0, keepdims=True)
+    for j in range(16):
+        tail[j, 0:1, :] = acc[:, j * dim : (j + 1) * dim]
+    finale = Hand(lambda j: tail.at[j], lambda j: tail_out.at[m, j], tsend, trecv)
+    finale.start()
+    tail_out[m, c] = tail[c]
+    spread.across(2)
+    spread.corner(1)
+    spread.across(3)
+    spread.corner(2)
+    spread.corner(3)
+    loads[3].wait()
+    for step in (1, 2, 3):
+        strip.ready(step)
+    strip_own = mixed_line.at[span((1 - m) * cut, cut), span(z * dim, dim)]
+    strip.landed(0, strip.PO, z, strip_own)
+    for step in range(4):
+        spread.ready(step)
+
+    value = contract_first(mixed_line[:, span(m * 256, 256)], ga_plane[...]).astype(BF)
+    for q in range(4):
+        out_mine[q] = value[:, q * dim : (q + 1) * dim]
+    high = lax.div(c, 8)
+    lower = lax.rem(s, 2)
+    cross = remote(out_mine, out_all.at[m], osend.at[0], orecv.at[0], pn)
+
+    def landing(q, core):
+        return out_grad.at[q, core]
+
+    def away(step, core):
+        q = (None, flip_x(s), flip_y(s), 3 - s)[step]
+        source = out_mine if core is None else out_all.at[1 - m]
+        who = m if core is None else 1 - m
+        at = step * 2 + (0 if core is None else 1)
+        return remote(source.at[q], landing(lower, who), osend.at[at], orecv.at[at], (q, z, m))
+
+    def lead():
+        for step in (1, 2, 3):
+            away(step, None).start()
+        out_grad[lower, m] = out_mine[s]
+        remote(out_all.at[1 - m], out_all.at[1 - m], osend.at[0], orecv.at[0], pn).wait_recv()
+        for step in (1, 2, 3):
+            away(step, 1).start()
+        out_grad[lower, 1 - m] = out_all[1 - m, s]
+    pl.when(high == m)(lead)
+    pl.when(high != m)(lambda: cross.start())
+    finale.collect()
+    pair_tail = remote(tail_out.at[m], tail_out.at[m], osend.at[8], orecv.at[8], pn)
+    pair_tail.start()
+    weights.collect()
+    for j in range(8):
+        for n, ref in enumerate((q_out, k_out, v_out)):
+            ref[:, pl.ds(j * dim, dim)] = got[j, :, pl.ds(n * dim, dim)].astype(F32)
+
+    def arrive(step):
+        q = (None, flip_x(s), flip_y(s), 3 - s)[step]
+
+        def take():
+            for second in (0, 1):
+                who = 1 - m if second else m
+                at = step * 2 + second
+                target = landing(lax.rem(q, 2), who)
+                remote(target, target, osend.at[at], orecv.at[at], pn).wait_recv()
+        pl.when(lax.div(q, 2) == m)(take)
+    for step in (1, 2, 3):
+        arrive(step)
+    other = tail_out.at[1 - m]
+    remote(other, other, osend.at[8], orecv.at[8], pn).wait_recv()
+    pair_tail.wait_send()
+    pl.when(high != m)(lambda: cross.wait_send())
+
+    def sent():
+        for step in (1, 2, 3):
+            away(step, None).wait_send()
+            away(step, 1).wait_send()
+    pl.when(high == m)(sent)
+    outer.landing()
+    for at in range(4):
+        pair(at, m).wait_send()
+    for work in (give, outer, inner, hand, finale, weights, strip, spread):
+        work.finish()
+
+
+def rear(ident, *arrays):
+    rows, width = arrays[0].shape
+    every = 16 * rows
+    cut = width // 2
+    vmem = pl.BlockSpec(memory_space=pltpu.VMEM)
+    hbm = pl.BlockSpec(memory_space=pl.ANY)
+    return pl.pallas_call(
+        rear_body,
+        out_shape=(
+            jax.ShapeDtypeStruct((rows, width), BF),
+            jax.ShapeDtypeStruct((rows, width), BF),
+            jax.ShapeDtypeStruct((rows, cut), F32),
+            jax.ShapeDtypeStruct((rows, cut), F32),
+            jax.ShapeDtypeStruct((rows, cut), F32),
+            jax.ShapeDtypeStruct((2, 2, 256, 128), BF),
+            jax.ShapeDtypeStruct((rows, width), F32),
+            jax.ShapeDtypeStruct((2, 16, 24, 128), F32),
+        ),
+        in_specs=[vmem] * 18 + [hbm] * 3,
+        out_specs=(vmem,) * 8,
+        scratch_shapes=[
+            pltpu.VMEM((8, rows, 384), BF),
+            pltpu.VMEM((rows, width), BF),
+            pltpu.VMEM((rows, width), F32),
+            pltpu.VMEM((cut, width), BF),
+            pltpu.VMEM((every, cut), BF),
+            pltpu.VMEM((every, width), BF),
+            pltpu.VMEM((every, cut), BF),
+            pltpu.VMEM((every, 512), BF),
+            pltpu.VMEM((4, rows, 512), BF),
+            pltpu.VMEM((every, 512), BF),
+            pltpu.VMEM((8, rows, 128), BF),
+            pltpu.VMEM((8, rows, 128), BF),
+            pltpu.VMEM((8, rows, 384), BF),
+            pltpu.VMEM((every, 384), BF),
+            pltpu.VMEM((every // 2, 128), F32),
+            pltpu.VMEM((every // 2, 128), F32),
+            pltpu.VMEM((every // 2, 128), F32),
+            pltpu.VMEM((16, 128), F32),
+            pltpu.VMEM((16, 16, 128), F32),
+            pltpu.VMEM((rows, 128), F32),
+            pltpu.VMEM((rows, 128), F32),
+            pltpu.VMEM((16, 24, 128), F32),
+            pltpu.VMEM((4, 256, 128), BF),
+            pltpu.VMEM((2, 4, 256, 128), BF),
+        ]
+        + reduce_buffers(True, rows, cut)
+        + reduce_buffers(False, rows, cut)
+        + [pltpu.SemaphoreType.DMA((1, 12, 4))] * 4
+        + [pltpu.SemaphoreType.DMA((16,))] * 4
+        + [pltpu.SemaphoreType.DMA((4,))] * 2
+        + [pltpu.SemaphoreType.DMA((9,))] * 2
+        + [pltpu.SemaphoreType.DMA((4,))]
+        + cores_semaphores()
+        + cores_semaphores(),
+        compiler_params=pltpu.CompilerParams(collective_id=ident, has_side_effects=True,
+                                             vmem_limit_bytes=66900000),
+        name="rear_%d" % ident,
+    )(*arrays)
+
 
 HEADS = 16
 HEAD_DIM = 128
@@ -52,7 +1532,7 @@
     return lax.psum(part.astype(jnp.bfloat16), "mp").astype(jnp.float32)
 
 
-def body(
+def general_body(
     tokens,
     positions,
     routes,
@@ -411,6 +1891,62 @@
     )
 
 
+def fast_body(
+    tokens, positions, routes, cotangent, attention_gain, query_weight, key_weight, value_weight,
+    query_gain, key_gain, output_weight, ffn_gain, router_weight, gate_weight, up_weight,
+    down_weight,
+):
+    s, z, m = place()
+    c = s * 4 + z
+    rows, width = tokens.shape[1:]
+    cut = width // 2
+    half = np.arange(HEAD_DIM // 2).astype(np.float32)
+    freq = np.float32(10000.0) ** (-(half * np.float32(2.0) / np.float32(HEAD_DIM)))
+    freq = jnp.asarray(np.tile(freq, (8, 2)), F32)
+    (normed, out_full, all_top, weights3, info, raw, rows3, squares, mixed, lse, trig, _, hidden,
+     normed_two, probs, chosen, share, head_gains, gains) = front(
+        0, tokens[0], attention_gain.reshape(1, rows), ffn_gain.reshape(1, rows), positions,
+        router_weight.T, query_gain, key_gain, routes[0], query_weight, key_weight, value_weight,
+        output_weight, cotangent[0], freq)
+    grad_two, prob_out, moe, gate_grad, up_grad, down_grad = experts(
+        5, normed_two, share, all_top, gate_weight[0], up_weight[0], down_weight[0])
+    _, moe_sum, query_grad, key_grad, value_grad, output_grad, tokens_grad, tail = rear(
+        6, grad_two, prob_out, probs, chosen, normed_two, hidden, cotangent[0], info,
+        mixed.reshape(8 * rows, HEAD_DIM), rows3, raw, squares, lse, trig, head_gains, weights3,
+        tokens[0], gains, out_full, normed, moe)
+    layer_output = (hidden + moe_sum.astype(F32)).astype(BF)
+    summed = jnp.sum(tail[0], axis=0)
+    gain_grads = lax.dynamic_slice_in_dim(tail[0] + tail[1], m * 8, 8, 0)
+    gain_grads = lax.dynamic_slice_in_dim(gain_grads, c * 8, 8, 2)
+    return (
+        layer_output[None],
+        tokens_grad[None],
+        summed[0],
+        query_grad,
+        key_grad,
+        value_grad,
+        gain_grads[:, 2],
+        gain_grads[:, 19],
+        output_grad.reshape(cut, HEAD_DIM).astype(F32),
+        summed[1],
+        summed[3:19].T,
+        gate_grad[None],
+        up_grad[None],
+        down_grad[None],
+    )
+
+
+def grid_fits(tokens, router_weight):
+    sizes = tuple(lax.axis_size(name) for name in ("seq", "ctx", "mp"))
+    return sizes == (4, 4, 2) and tokens.shape == (1, 128, 2048) and router_weight.shape == (128, 16)
+
+
+def body(*args):
+    if grid_fits(args[0], args[12]):
+        return fast_body(*args)
+    return general_body(*args)
+
+
 def solution(mesh):
     placed = (
         P("seq", "ctx", None),

time: 2050 us -> 431 us (0.21)
  waiting for transfers between devices: 1280 us -> 0 us
  Pallas kernels: 0 us -> 403 us
  blocking collectives: 401 us -> 0 us
  matrix products: 127 us -> 0 us
  other arithmetic: 72.8 us -> 5.72 us
  local copies, waits for them, and re-layouts: 82.7 us -> 16.2 us
  starting transfers between devices: 60.2 us -> 0 us
    reduce_scatter x5 -> x0, waiting for transfers between devices: 701 us -> none  [the longest x1 183 us: body(): lax.psum_scatter(value_grad, ('seq', 'ctx'), scatter_dimension=0, tiled=T...]
    pallas_call x0 -> x3, Pallas kernels: none -> 403 us  [the longest x1 149 us: rear(): pl.pallas_call(rear_body, out_shape=(jax.ShapeDtypeStruct((rows, width),...]
    all_to_all x3 -> x0, waiting for transfers between devices: 321 us -> none  [the longest x1 122 us: body(): lax.all_to_all(grad_slots, ('seq', 'ctx'), split_axis=0, concat_axis=0, t...]
    all_gather x5 -> x0, blocking collectives: 188 us -> none  [the longest x1 41.2 us: body(): lax.all_gather(key_gain, ('seq', 'ctx'), axis=1, tiled=True)]
    all_gather x6 -> x0, waiting for transfers between devices: 182 us -> none  [the longest x1 74.4 us: body(): lax.all_gather(output_weight, ('seq', 'ctx'), axis=1, tiled=True)]
    all_to_all x1 -> x0, blocking collectives: 136 us -> none  [body(): lax.all_to_all(outgoing, ('seq', 'ctx'), split_axis=0, concat_axis=0, til...]
    dot_general x31 -> x0, matrix products: 127 us -> none  [the longest x8 40.3 us: contract_first(): lax.dot_general(left, right, (((0,), (0,)), ((), ())), preferred_element_...]
    unnamed x1 -> x0, blocking collectives: 71.8 us -> none
  transfers between devices with their start and end apart: 20 -> 0, of which waited for: 13 -> 0; matrix products, arithmetic and copies ran while one was open for 9% -> 0% of each run, Pallas kernels for 0% -> 0%
where the time goes in v1:
time: 431 us; the launch traced here: 426 us
  Pallas kernels  403 us (94%)
  local copies, waits for them, and re-layouts  16.2 us (4%)
  other arithmetic  5.72 us (1%)
    pallas_call x1, Pallas kernels, rear(): pl.pallas_call(rear_body, out_shape=(jax.ShapeDtypeStruct((rows, width),...  149 us
    pallas_call x1, Pallas kernels, front(): pl.pallas_call(front_body, out_shape=(shape(every, width, dtype=BF), shap...  148 us
    pallas_call x1, Pallas kernels, experts(): pl.pallas_call(experts_body, out_shape=(jax.ShapeDtypeStruct((rows, width...  107 us
    unnamed x22, local copies, waits for them, and re-layouts  14.2 us

profile of v1, /device:TPU:12, one launch (start us, length us, event | category | flops | bytes accessed | tf_op | source)
XLA Modules:
  0.0 426.4 jit_solution(16171173025440135155)
XLA Ops:
  0.6 1.4 copy.34
  2.1 148.2 %front_0.1 = (bf16[2048,2048]{1,0:T(8,128)(2,1)}, bf16[2048,2048]{1,0:T(8,128)(2,1)}, bf16[2048,2048]{1,0:T(8,128)(2,1)}, bf16[16,128,384]{2,1,0:T(8,128)(2,1)},...) custom-call(bf16[128,2048]{1,0:T(8,128)(2,1)} %bitcast.29, ...), custom_call_target="tpu_custom_call" | custom-call | tf_op jit(solution)/shard_map/front_0/pallas_call | solution.py:1015
  150.2 106.6 %experts_5.1 = (bf16[128,2048]{1,0:T(8,128)(2,1)}, f32[2,16,8,128]{3,2,1,0:T(8,128)}, bf16[2048,2048]{1,0:T(8,128)(2,1)}, f32[2048,512]{1,0:T(8,128)}, f32[2048,512]{1,0:T(8,128)}, /*index=5*/f32[512,2048]{1,0:T(8,128)}) custom-call(bf16[128,2048]{1,0:T(8,128)(2,1)} %get-tuple-element.46.two_ref, f32[16,128]{1,0:T(8,128)} %get-tuple-element.47.share_ref, ...), custom_call_target="tpu_custom_call" | custom-call | tf_op jit(solution)/shard_map/experts_5/pallas_call | solution.py:638
  256.8 148.7 %rear_6.1 = (bf16[128,2048]{1,0:T(8,128)(2,1)}, bf16[128,2048]{1,0:T(8,128)(2,1)}, f32[128,1024]{1,0:T(8,128)}, f32[128,1024]{1,0:T(8,128)}, f32[128,1024]{1,0:T...) custom-call(bf16[128,2048]{1,0:T(8,128)(2,1)} %get-tuple-element.49.back_ref, ...), custom_call_target="tpu_custom_call" | custom-call | tf_op jit(solution)/shard_map/rear_6/pallas_call | solution.py:1431
  405.6 0.0 copy-start.3
  405.6 0.0 copy-start.6
  405.6 0.0 copy-start.5
  405.6 0.0 copy-start.4
  405.6 1.2 fusion.1
  406.8 0.1 dynamic-slice_add_fusion
  407.0 0.1 copy.35
  407.0 0.0 copy-start.2
  407.0 0.8 slice_reduce_fusion
  407.8 2.1 bitcast_convert_fusion
  409.9 2.3 fusion
  412.2 0.6 slice_bitcast_fusion
  412.8 0.5 slice_bitcast_fusion.1
  413.3 0.0 copy-done.3
  413.3 1.0 copy.43
  414.3 0.0 copy-done.6
  414.3 0.8 copy.44
  415.1 0.0 copy-done.5
  415.1 0.8 copy.45
  415.9 0.0 copy-done.4
  415.9 0.8 copy.46
  416.7 0.0 copy-done.2
  416.7 0.0 copy-start.1
  416.7 2.1 copy.47
  418.8 1.6 copy-done.1
  420.4 0.0 copy-start
  420.4 2.1 copy.48
  422.5 1.6 copy-done
  424.1 2.0 copy.49
Async XLA Ops:
  405.6 7.7 %copy-start.3 = (f32[128,2048]{1,0:T(8,128)S(1)}, f32[128,2048]{1,0:T(8,128)}, u32[]{:S(2)}) copy-start(f32[128,2048]{1,0:T(8,128)} %get-tuple-element.67) | copy-start | bytes 3145732
  405.6 8.7 %copy-start.6 = (f32[128,1024]{1,0:T(8,128)S(1)}, f32[128,1024]{1,0:T(8,128)}, u32[]{:S(2)}) copy-start(f32[128,1024]{1,0:T(8,128)} %get-tuple-element.100) | copy-start | bytes 1572868
  405.6 9.5 %copy-start.5 = (f32[128,1024]{1,0:T(8,128)S(1)}, f32[128,1024]{1,0:T(8,128)}, u32[]{:S(2)}) copy-start(f32[128,1024]{1,0:T(8,128)} %get-tuple-element.101) | copy-start | bytes 1572868
  405.6 10.3 %copy-start.4 = (f32[128,1024]{1,0:T(8,128)S(1)}, f32[128,1024]{1,0:T(8,128)}, u32[]{:S(2)}) copy-start(f32[128,1024]{1,0:T(8,128)} %get-tuple-element.102) | copy-start | bytes 1572868
  407.0 9.6 %copy-start.2 = (f32[2048,512]{1,0:T(8,128)S(1)}, f32[2048,512]{1,0:T(8,128)}, u32[]{:S(2)}) copy-start(f32[2048,512]{1,0:T(8,128)} %get-tuple-element.73) | copy-start | bytes 12582916
  416.7 3.7 copy-start.1
  420.4 3.7 copy-start

commit v2 on v1

--- a/solution.py
+++ b/solution.py
@@ -235,14 +235,13 @@
         self.push(True, 0, self.PO, at, target, target, self.pn)
 
 
-def meet_chips():
+def call_chips():
     s, z, m = place()
     c = s * 4 + z
     for step in range(1, 16):
         j = lax.rem(c + step, 16)
         signal((lax.div(j, 4), lax.rem(j, 4), m))
     signal((s, z, 1 - m))
-    pl.semaphore_wait(pltpu.get_barrier_semaphore(), 16)
 
 
 def add_rows(put, sources, count, step=16):
@@ -430,7 +429,8 @@
     ]
     for copy in loads:
         copy.start()
-    meet_chips()
+    call_chips()
+    pl.semaphore_wait(pltpu.get_barrier_semaphore(), 16)
     work = Gather([Part("rows", two_ref, two_all), Part("small", share_ref, shares)], gsend, grecv)
     work.start()
     two_all[span((z * 4 + s) * rows, rows), :] = two_ref[...]
@@ -778,6 +778,7 @@
     dim = 128
     planes = near_planes(z)
     lane = lax.broadcasted_iota(jnp.int32, (rows, dim), 1)
+    call_chips()
     info_ref[...] = jnp.zeros_like(info_ref)
     info_ref[0:1, :] = one_ref[...].astype(F32)
     info_ref[1:2, :] = second_ref[...].astype(F32)
@@ -788,11 +789,13 @@
     for i in range(8):
         for n, ref in enumerate((qw_ref, kw_ref, vw_ref)):
             packed_ref[i, :, pl.ds(n * dim, dim)] = ref[:, pl.ds(i * dim, dim)]
-    meet_chips()
+    pl.semaphore_wait(pltpu.get_barrier_semaphore(), 16)
     hand = Hand(lambda j: info_ref, lambda j: info.at[m, j], isend, irecv)
     hand.start()
     weights = Chips(lambda i: packed_ref.at[i], w3, *chips_sems[:5])
     weights.start()
+    outer = Gather([Part("heads", wo_ref, wo_all)], osend, orecv)
+    outer.start()
     info[m, c] = info_ref[...]
 
     def square_sum(r, _):
@@ -847,8 +850,8 @@
     project(0)
     first.corner(1)
     first.across(3)
-    outer = Gather([Part("heads", wo_ref, wo_all)], osend, orecv)
-    outer.start()
+    outer.along(1)
+    outer.across(0)
     first.ready(1)
     project(1)
     first.corner(2)
@@ -873,6 +876,7 @@
     save_n1.start()
     wo_own = pltpu.make_async_copy(wo_ref, outer.parts[0].piece(s, z, m), pairs.at[3])
     wo_own.start()
+    outer.along(2)
     share.collect()
 
     def add_up(j, acc):
@@ -881,7 +885,6 @@
     squares[...] = summed
     wide = jnp.concatenate([lax.rsqrt(summed / width + eps), jnp.zeros((rows - 16, dim), F32)], axis=0)
     line[...] = jnp.transpose(wide)
-    outer.along(1)
 
     def head_gain(which):
         total = jnp.zeros((8, dim), F32)
@@ -904,8 +907,8 @@
             rows3[at, pl.ds(which * dim, dim)] = (value * factor).astype(BF)
         return 0
     lax.fori_loop(0, 8, turn, 0)
-    outer.across(0)
-    outer.along(2)
+    outer.across(1)
+    outer.along(3)
 
     def attend(b, _):
         seq = span(lax.div(b, 4) * 4 * rows, 4 * rows)
@@ -924,8 +927,6 @@
     lax.fori_loop(0, 8, attend, 0)
     back = Chips(lambda i: mixed.at[i], own_mixed, *chips_sems[5:])
     back.start()
-    outer.across(1)
-    outer.along(3)
     outer.corner(0)
     outer.across(2)
     back.collect()
@@ -1104,21 +1105,22 @@
     return [pltpu.SemaphoreType.DMA((8,))] * 2 + [pltpu.SemaphoreType.DMA((1,))]
 
 
-def meet_all():
+def call_all():
     s, z, m = place()
-    c = s * 4 + z
-    high = lax.div(c, 8)
-    for step in range(1, 16):
-        j = lax.rem(c + step, 16)
-        signal((lax.div(j, 4), lax.rem(j, 4), m))
-    signal((s, z, 1 - m))
+    high = lax.div(s * 4 + z, 8)
+    call_chips()
 
     def cross():
         for i in range(8):
             j = 8 * m + i
             signal((lax.div(j, 4), lax.rem(j, 4), high))
-        pl.semaphore_wait(pltpu.get_barrier_semaphore(), 24)
     pl.when(high != m)(cross)
+
+
+def await_all():
+    s, z, m = place()
+    high = lax.div(s * 4 + z, 8)
+    pl.when(high != m)(lambda: pl.semaphore_wait(pltpu.get_barrier_semaphore(), 24))
     pl.when(high == m)(lambda: pl.semaphore_wait(pltpu.get_barrier_semaphore(), 16))
 
 
@@ -1146,6 +1148,10 @@
     ]
     for copy in loads:
         copy.start()
+    call_all()
+    order = far_planes(z)
+    outer = Reduce(True, True, moe, moe, moe_out, (a0, a1, a2, a3, a4, a5, a6, a7), (asend, arecv))
+    inner = Reduce(False, True, gn_part, gn_part, gn_out, (b0, b1, b2, b3, b4, b5, b6, b7), (bsend, brecv))
     prob = jnp.concatenate(
         [prob_ref[0, j, 0:1, :] + prob_ref[1, j, 0:1, :] for j in range(16)], axis=0)
     prob = prob * chosen_ref[...]
@@ -1175,9 +1181,11 @@
     acc = jnp.sum(acc, axis=0, keepdims=True)
     for j in range(16):
         tail[j, 1:2, :] = acc[:, j * dim : (j + 1) * dim]
-    meet_all()
+    await_all()
+    loads[1].wait()
+    for at in order:
+        outer.swap(at)
     lane = lax.broadcasted_iota(jnp.int32, (rows, dim), 1)
-    order = far_planes(z)
     give = Cores(gm_send, gm, *rest[:3])
     loads[0].wait()
     for t in range(2):
@@ -1187,11 +1195,6 @@
         give.start(t * 4, t * 4 + 4)
     strip = Line([Part("line", mixed_ref, mixed_line)], msend, mrecv)
     spread = Spread([Part("cols", ga_blocks, ga_plane)], csend, crecv)
-    loads[1].wait()
-    outer = Reduce(True, True, moe, moe, moe_out, (a0, a1, a2, a3, a4, a5, a6, a7), (asend, arecv))
-    inner = Reduce(False, True, gn_part, gn_part, gn_out, (b0, b1, b2, b3, b4, b5, b6, b7), (bsend, brecv))
-    for at in order:
-        outer.swap(at)
 
     wide = jnp.concatenate(
         [lax.rsqrt(squares[...] / width + eps), jnp.zeros((rows - 16, dim), F32)], axis=0)

time: 431 us -> 422 us (0.979)
  Pallas kernels: 403 us -> 395 us
where the time goes in v2:
time: 422 us; the launch traced here: 418 us
  Pallas kernels  395 us (94%)
  local copies, waits for them, and re-layouts  16.2 us (4%)
  other arithmetic  5.72 us (1%)
    pallas_call x1, Pallas kernels, rear(): pl.pallas_call(rear_body, out_shape=(jax.ShapeDtypeStruct((rows, width),...  146 us
    pallas_call x1, Pallas kernels, front(): pl.pallas_call(front_body, out_shape=(shape(every, width, dtype=BF), shap...  144 us
    pallas_call x1, Pallas kernels, experts(): pl.pallas_call(experts_body, out_shape=(jax.ShapeDtypeStruct((rows, width...  104 us
    unnamed x22, local copies, waits for them, and re-layouts  14.2 us

profile of v2, /device:TPU:12, one launch (start us, length us, event | category | flops | bytes accessed | tf_op | source)
XLA Modules:
  0.0 417.8 jit_solution(18396759639674814459)
XLA Ops:
  0.6 1.4 copy.34
  2.1 144.5 %front_0.1 = (bf16[2048,2048]{1,0:T(8,128)(2,1)}, bf16[2048,2048]{1,0:T(8,128)(2,1)}, bf16[2048,2048]{1,0:T(8,128)(2,1)}, bf16[16,128,384]{2,1,0:T(8,128)(2,1)},...) custom-call(bf16[128,2048]{1,0:T(8,128)(2,1)} %bitcast.29, ...), custom_call_target="tpu_custom_call" | custom-call | tf_op jit(solution)/shard_map/front_0/pallas_call | solution.py:1016
  146.5 104.1 %experts_5.1 = (bf16[128,2048]{1,0:T(8,128)(2,1)}, f32[2,16,8,128]{3,2,1,0:T(8,128)}, bf16[2048,2048]{1,0:T(8,128)(2,1)}, f32[2048,512]{1,0:T(8,128)}, f32[2048,512]{1,0:T(8,128)}, /*index=5*/f32[512,2048]{1,0:T(8,128)}) custom-call(bf16[128,2048]{1,0:T(8,128)(2,1)} %get-tuple-element.46.two_ref, f32[16,128]{1,0:T(8,128)} %get-tuple-element.47.share_ref, ...), custom_call_target="tpu_custom_call" | custom-call | tf_op jit(solution)/shard_map/experts_5/pallas_call | solution.py:638
  250.6 146.4 %rear_6.1 = (bf16[128,2048]{1,0:T(8,128)(2,1)}, bf16[128,2048]{1,0:T(8,128)(2,1)}, f32[128,1024]{1,0:T(8,128)}, f32[128,1024]{1,0:T(8,128)}, f32[128,1024]{1,0:T...) custom-call(bf16[128,2048]{1,0:T(8,128)(2,1)} %get-tuple-element.49.back_ref, ...), custom_call_target="tpu_custom_call" | custom-call | tf_op jit(solution)/shard_map/rear_6/pallas_call | solution.py:1434
  397.0 0.0 copy-start.3
  397.0 0.0 copy-start.6
  397.0 0.0 copy-start.5
  397.0 0.0 copy-start.4
  397.1 1.2 fusion.1
  398.3 0.1 dynamic-slice_add_fusion
  398.4 0.1 copy.35
  398.5 0.0 copy-start.2
  398.5 0.8 slice_reduce_fusion
  399.2 2.1 bitcast_convert_fusion
  401.4 2.3 fusion
  403.6 0.6 slice_bitcast_fusion
  404.2 0.5 slice_bitcast_fusion.1
  404.8 0.0 copy-done.3
  404.8 1.0 copy.43
  405.7 0.0 copy-done.6
  405.7 0.8 copy.44
  406.5 0.0 copy-done.5
  406.5 0.8 copy.45
  407.3 0.0 copy-done.4
  407.3 0.8 copy.46
  408.1 0.0 copy-done.2
  408.1 0.0 copy-start.1
  408.1 2.1 copy.47
  410.3 1.6 copy-done.1
  411.8 0.0 copy-start
  411.8 2.1 copy.48
  414.0 1.6 copy-done
  415.5 2.0 copy.49
Async XLA Ops:
  397.0 7.7 %copy-start.3 = (f32[128,2048]{1,0:T(8,128)S(1)}, f32[128,2048]{1,0:T(8,128)}, u32[]{:S(2)}) copy-start(f32[128,2048]{1,0:T(8,128)} %get-tuple-element.67) | copy-start | bytes 3145732
  397.0 8.7 %copy-start.6 = (f32[128,1024]{1,0:T(8,128)S(1)}, f32[128,1024]{1,0:T(8,128)}, u32[]{:S(2)}) copy-start(f32[128,1024]{1,0:T(8,128)} %get-tuple-element.100) | copy-start | bytes 1572868
  397.0 9.5 %copy-start.5 = (f32[128,1024]{1,0:T(8,128)S(1)}, f32[128,1024]{1,0:T(8,128)}, u32[]{:S(2)}) copy-start(f32[128,1024]{1,0:T(8,128)} %get-tuple-element.101) | copy-start | bytes 1572868
  397.0 10.3 %copy-start.4 = (f32[128,1024]{1,0:T(8,128)S(1)}, f32[128,1024]{1,0:T(8,128)}, u32[]{:S(2)}) copy-start(f32[128,1024]{1,0:T(8,128)} %get-tuple-element.102) | copy-start | bytes 1572868
  398.5 9.6 %copy-start.2 = (f32[2048,512]{1,0:T(8,128)S(1)}, f32[2048,512]{1,0:T(8,128)}, u32[]{:S(2)}) copy-start(f32[2048,512]{1,0:T(8,128)} %get-tuple-element.73) | copy-start | bytes 12582916
  408.1 3.7 copy-start.1
  411.8 3.7 copy-start

commit v3 on v2

--- a/solution.py
+++ b/solution.py
@@ -450,7 +450,7 @@
 
         def tile(cols):
             pull[at, cols] = contract_last(top_all[at, :], down_w[cols, :])
-        tiles(hidden, 512, tile)
+        tiles(hidden, 256, tile)
 
     def enter(side, k):
         at = span(planes[k] * block, block)
@@ -483,22 +483,24 @@
 
         def tile(cols):
             back[at, cols] = contract_last(dpair[at, :], pair_w[cols, :]).astype(BF)
-        tiles(width, 1024, tile)
+        tiles(width, 512, tile)
         total.swap(planes[k])
 
     def saves(i, t):
-        cols = pl.ds(t * 1024, 1024)
         return pltpu.make_async_copy(
-            stage.at[t], moe_out.at[pl.ds(i * block, block), cols], store.at[t])
+            stage.at[t], moe_out.at[pl.ds(i * block, block), span(t * 1024, 1024)], store.at[t])
 
     def moes(i):
         at = pl.ds(i * block, block)
-        for t in (0, 1):
+
+        def one(t, _):
             if i >= 1:
                 saves(i - 1, t).wait()
-            cols = pl.ds(t * 1024, 1024)
+            cols = span(t * 1024, 1024)
             stage[t] = jnp.dot(acts[at, :], down_w[:, cols], preferred_element_type=F32).astype(BF)
             saves(i, t).start()
+            return 0
+        lax.fori_loop(0, 2, one, 0)
 
     def keep(i):
         rows_at = span(i * 512, 512)
@@ -514,7 +516,7 @@
 
     def keep_down(i):
         return pltpu.make_async_copy(
-            dstage.at[i], ddown_out.at[:, pl.ds(i * 1024, 1024)], dstore.at[i, 2])
+            dstage.at[i], ddown_out.at[:, span(i * 1024, 1024)], dstore.at[i, 2])
 
     def grads(low, high):
         def one(i, _):
@@ -523,7 +525,12 @@
                     copy.wait()
             pl.when(i >= 2)(settle)
             cols = span(i * 512, 512)
-            dstage[lax.rem(i, 2)] = contract_first(two_all[:, cols], dpair[...])
+
+            def side(n, _):
+                here = span(n * hidden, hidden)
+                dstage[lax.rem(i, 2), :, here] = contract_first(two_all[:, cols], dpair[:, here])
+                return 0
+            lax.fori_loop(0, 2, side, 0)
             for copy in keep(i):
                 copy.start()
             return 0
@@ -533,9 +540,12 @@
         for i in (2, 3):
             for copy in keep(i):
                 copy.wait()
-        for i in (0, 1):
-            dstage[i] = contract_first(acts[...], top_all[:, pl.ds(i * 1024, 1024)])
+
+        def one(i, _):
+            dstage[i] = contract_first(acts[...], top_all[:, span(i * 1024, 1024)])
             keep_down(i).start()
+            return 0
+        lax.fori_loop(0, 2, one, 0)
 
     loads[0].wait()
     loads[1].wait()
@@ -604,14 +614,13 @@
     moes(3)
     grads(0, 1)
     total.third(planes[3], 2)
-    grads(1, 3)
     for step in range(1, 16):
         j = lax.rem(c + 16 - step, 16)
         target = prob_out.at[m, j]
         remote(target, target, psend.at[step], precv.at[step], dev(j)).wait_recv()
     pair = remote(prob_out.at[m], prob_out.at[m], psend.at[0], precv.at[0], (s, z, 1 - m))
     pair.start()
-    grads(3, 4)
+    grads(1, 4)
     downs()
     total.close()
     for i in (0, 1):
@@ -840,13 +849,14 @@
     first.ready(0)
 
     def project(k):
-        value = jnp.dot(n1_all[span((planes[k] * 4 + 2 * m) * rows, 2 * rows), :],
-                        w3[...].reshape(width, 3 * dim), preferred_element_type=F32)
-        for e in (0, 1):
-            part = value[e * rows : (e + 1) * rows, :]
+        def one(e, _):
+            value = jnp.dot(n1_all[span((planes[k] * 4 + 2 * m + e) * rows, rows), :],
+                            w3[...].reshape(width, 3 * dim), preferred_element_type=F32)
             base = span((e * 4 + planes[k]) * rows, rows)
-            raw[base, :] = part[:, : 2 * dim]
-            rows3[base, pl.ds(2 * dim, dim)] = part[:, 2 * dim :].astype(BF)
+            raw[base, :] = value[:, : 2 * dim]
+            rows3[base, pl.ds(2 * dim, dim)] = value[:, 2 * dim :].astype(BF)
+            return 0
+        lax.fori_loop(0, 2, one, 0)
     project(0)
     first.corner(1)
     first.across(3)
@@ -1188,11 +1198,13 @@
     lane = lax.broadcasted_iota(jnp.int32, (rows, dim), 1)
     give = Cores(gm_send, gm, *rest[:3])
     loads[0].wait()
-    for t in range(2):
-        value = contract_last(ga_ref[...], wo_half[pl.ds(t * 512, 512), :]).astype(BF)
+    def mix(t, _):
+        value = contract_last(ga_ref[...], wo_half[span(t * 512, 512), :]).astype(BF)
         for i in range(4):
             gm_send[t * 4 + i] = value[:, i * dim : (i + 1) * dim]
-        give.start(t * 4, t * 4 + 4)
+        return 0
+    lax.fori_loop(0, 2, mix, 0)
+    give.start()
     strip = Line([Part("line", mixed_ref, mixed_line)], msend, mrecv)
     spread = Spread([Part("cols", ga_blocks, ga_plane)], csend, crecv)
 
@@ -1293,19 +1305,23 @@
     for at in range(4):
         pair(at, 1 - m).wait_recv()
     for at in order:
-        here = span(at * 4 * rows, 4 * rows)
-        gn_part[here, :] = contract_last(
-            backs[here, :], w3[span(m * 8, 8)].reshape(cut, 3 * dim)).astype(BF)
+        def chunk(t, _, at=at):
+            here = span((at * 2 + t) * 2 * rows, 2 * rows)
+            gn_part[here, :] = contract_last(
+                backs[here, :], w3[span(m * 8, 8)].reshape(cut, 3 * dim)).astype(BF)
+            return 0
+        lax.fori_loop(0, 2, chunk, 0)
         inner.first(at)
     outer.keep()
     strip.along(1)
     spread.along(1)
     loads[2].wait()
 
-    def weight_tile(t):
-        value = contract_first(n1_half[:, pl.ds(t * 256, 256)], backs[...]).astype(BF)
-        wsend[2 * t] = value[:rows]
-        wsend[2 * t + 1] = value[rows:]
+    def weight_tile(n):
+        def one(t, _):
+            wsend[t] = contract_first(n1_half[:, span(t * dim, dim)], backs[...]).astype(BF)
+            return 0
+        lax.fori_loop(2 * n, 2 * n + 2, one, 0)
     weight_tile(0)
     weight_tile(1)
     inner.second(order[0])

time: 422 us -> 418 us (level)
  no operation moved by 1% of the time
where the time goes in v3:
time: 418 us; the launch traced here: 417 us
  Pallas kernels  395 us (94%)
  local copies, waits for them, and re-layouts  16.2 us (4%)
  other arithmetic  5.72 us (1%)
    pallas_call x1, Pallas kernels, rear(): pl.pallas_call(rear_body, out_shape=(jax.ShapeDtypeStruct((rows, width),...  146 us
    pallas_call x1, Pallas kernels, front(): pl.pallas_call(front_body, out_shape=(shape(every, width, dtype=BF), shap...  144 us
    pallas_call x1, Pallas kernels, experts(): pl.pallas_call(experts_body, out_shape=(jax.ShapeDtypeStruct((rows, width...  104 us
    unnamed x22, local copies, waits for them, and re-layouts  14.2 us

profile of v3, /device:TPU:12, one launch (start us, length us, event | category | flops | bytes accessed | tf_op | source)
XLA Modules:
  0.0 417.3 jit_solution(2688592498184963164)
XLA Ops:
  0.6 1.4 copy.34
  2.1 144.4 %front_0.1 = (bf16[2048,2048]{1,0:T(8,128)(2,1)}, bf16[2048,2048]{1,0:T(8,128)(2,1)}, bf16[2048,2048]{1,0:T(8,128)(2,1)}, bf16[16,128,384]{2,1,0:T(8,128)(2,1)},...) custom-call(bf16[128,2048]{1,0:T(8,128)(2,1)} %bitcast.29, ...), custom_call_target="tpu_custom_call" | custom-call | tf_op jit(solution)/shard_map/front_0/pallas_call | solution.py:1026
  146.5 104.5 %experts_5.1 = (bf16[128,2048]{1,0:T(8,128)(2,1)}, f32[2,16,8,128]{3,2,1,0:T(8,128)}, bf16[2048,2048]{1,0:T(8,128)(2,1)}, f32[2048,512]{1,0:T(8,128)}, f32[2048,512]{1,0:T(8,128)}, /*index=5*/f32[512,2048]{1,0:T(8,128)}) custom-call(bf16[128,2048]{1,0:T(8,128)(2,1)} %get-tuple-element.46.two_ref, f32[16,128]{1,0:T(8,128)} %get-tuple-element.47.share_ref, ...), custom_call_target="tpu_custom_call" | custom-call | tf_op jit(solution)/shard_map/experts_5/pallas_call | solution.py:647
  251.0 145.8 %rear_6.1 = (bf16[128,2048]{1,0:T(8,128)(2,1)}, bf16[128,2048]{1,0:T(8,128)(2,1)}, f32[128,1024]{1,0:T(8,128)}, f32[128,1024]{1,0:T(8,128)}, f32[128,1024]{1,0:T...) custom-call(bf16[128,2048]{1,0:T(8,128)(2,1)} %get-tuple-element.49.back_ref, ...), custom_call_target="tpu_custom_call" | custom-call | tf_op jit(solution)/shard_map/rear_6/pallas_call | solution.py:1450
  396.8 0.0 copy-start.3
  396.8 0.0 copy-start.6
  396.8 0.0 copy-start.5
  396.8 0.0 copy-start.4
  396.8 1.2 fusion.1
  398.1 0.1 dynamic-slice_add_fusion
  398.2 0.1 copy.35
  398.3 0.0 copy-start.2
  398.3 0.8 slice_reduce_fusion
  399.0 2.1 bitcast_convert_fusion
  401.2 2.3 fusion
  403.4 0.6 slice_bitcast_fusion
  404.0 0.5 slice_bitcast_fusion.1
  404.5 0.0 copy-done.3
  404.6 1.0 copy.43
  405.5 0.0 copy-done.6
  405.5 0.8 copy.44
  406.3 0.0 copy-done.5
  406.3 0.8 copy.45
  407.1 0.0 copy-done.4
  407.1 0.8 copy.46
  407.9 0.0 copy-done.2
  407.9 0.0 copy-start.1
  407.9 2.1 copy.47
  410.1 1.6 copy-done.1
  411.6 0.0 copy-start
  411.6 2.1 copy.48
  413.8 1.6 copy-done
  415.3 2.0 copy.49
Async XLA Ops:
  396.8 7.7 %copy-start.3 = (f32[128,2048]{1,0:T(8,128)S(1)}, f32[128,2048]{1,0:T(8,128)}, u32[]{:S(2)}) copy-start(f32[128,2048]{1,0:T(8,128)} %get-tuple-element.67) | copy-start | bytes 3145732
  396.8 8.7 %copy-start.6 = (f32[128,1024]{1,0:T(8,128)S(1)}, f32[128,1024]{1,0:T(8,128)}, u32[]{:S(2)}) copy-start(f32[128,1024]{1,0:T(8,128)} %get-tuple-element.100) | copy-start | bytes 1572868
  396.8 9.5 %copy-start.5 = (f32[128,1024]{1,0:T(8,128)S(1)}, f32[128,1024]{1,0:T(8,128)}, u32[]{:S(2)}) copy-start(f32[128,1024]{1,0:T(8,128)} %get-tuple-element.101) | copy-start | bytes 1572868
  396.8 10.3 %copy-start.4 = (f32[128,1024]{1,0:T(8,128)S(1)}, f32[128,1024]{1,0:T(8,128)}, u32[]{:S(2)}) copy-start(f32[128,1024]{1,0:T(8,128)} %get-tuple-element.102) | copy-start | bytes 1572868
  398.3 9.6 %copy-start.2 = (f32[2048,512]{1,0:T(8,128)S(1)}, f32[2048,512]{1,0:T(8,128)}, u32[]{:S(2)}) copy-start(f32[2048,512]{1,0:T(8,128)} %get-tuple-element.73) | copy-start | bytes 12582916
  407.9 3.7 copy-start.1
  411.6 3.7 copy-start
